TPU v7x, 64 devices: a 2x2x8 block of a 4x4x8 slice. The times are simulated.
64 devices in a mesh: dp: 4 (over x, y), dap: 16 (over z, core).
Axes of the slice: x: 2, y: 2, z: 8, core: 2. Of those that a mesh axis runs over, the one named last changes fastest.
The devices are a block of a 4x4x8 slice.
Arguments:
- z: bfloat16 [512, 128, 128], P(('dp', 'dap')), parts along dimension 0
- pair_mask: int32 [512, 128], P(('dp', 'dap')), parts along dimension 0
- dz_out: bfloat16 [512, 128, 128], P(('dp', 'dap')), parts along dimension 0
- ln_scale: float32 [2, 128], replicated
- ln_shift: float32 [2, 128], replicated
- w_proj: bfloat16 [2, 128, 512], replicated
- w_bias: bfloat16 [2, 128, 4], replicated
- b_gate: float32 [2, 128], replicated
- w_out: bfloat16 [2, 128, 128], replicated
- b_out: float32 [2, 128], replicated
Outputs:
- output 1: bfloat16 [512, 128, 128], P(('dp', 'dap')), parts along dimension 0
- output 2: bfloat16 [512, 128, 128], P(('dp', 'dap')), parts along dimension 0
- output 3: float32 [8, 128], P('dp'), parts along dimension 0
- output 4: float32 [8, 128], P('dp'), parts along dimension 0
- output 5: float32 [8, 128, 512], P('dp'), parts along dimension 0
- output 6: float32 [8, 128, 4], P('dp'), parts along dimension 0
- output 7: float32 [8, 128], P('dp'), parts along dimension 0
- output 8: float32 [8, 128, 128], P('dp'), parts along dimension 0
- output 9: float32 [8, 128], P('dp'), parts along dimension 0
There are 4 independent parts. A program takes and returns all parts, laid end to end along the dimension named above; an argument that names none is the same for every part.
All inputs are finite; a program needn't handle non-finite values.
Results may differ from a plain program's by a relative error of at most 0.02.
Values are sent between devices in bfloat16 or wider.
A program may use at most 768 MiB of HBM per device.

v0:
```python
import jax
import jax.numpy as jnp
from jax import lax
from jax.sharding import PartitionSpec as P

EPS = 1e-5
MASK_FILL = 1e9


def layer_norm(pair_in, ln_gain, ln_bias):
    wide = pair_in.astype(jnp.float32)
    centred = wide - jnp.mean(wide, axis=-1, keepdims=True)
    inv_std = lax.rsqrt(jnp.mean(centred * centred, axis=-1, keepdims=True) + EPS)
    x_hat = centred * inv_std
    return (x_hat * ln_gain + ln_bias).astype(jnp.bfloat16), x_hat, inv_std


def layer_norm_bwd(d_normed, x_hat, inv_std, ln_gain):
    d_hat = d_normed * ln_gain
    d_in = inv_std * (d_hat - jnp.mean(d_hat, axis=-1, keepdims=True) - x_hat * jnp.mean(d_hat * x_hat, axis=-1, keepdims=True))
    return d_in, jnp.sum(d_normed * x_hat, axis=(0, 1)), jnp.sum(d_normed, axis=(0, 1))


def row_probs(heads_row, mask_row, tri_bias, logit_scale):
    logits = jnp.einsum('jhd,khd->hjk', heads_row[:, 0], heads_row[:, 1], preferred_element_type=jnp.float32)
    return jax.nn.softmax(logits * logit_scale + tri_bias + mask_row, axis=-1)


def attend(qkvg, mask_bias, tri_bias, logit_scale):
    def one_row(row_args):
        heads_row, mask_row = row_args
        att_probs = row_probs(heads_row, mask_row, tri_bias, logit_scale)
        return jnp.einsum('hjk,khd->jhd', att_probs.astype(jnp.bfloat16), heads_row[:, 2], preferred_element_type=jnp.float32)
    return lax.map(one_row, (qkvg, mask_bias))


def attend_bwd(qkvg, mask_bias, tri_bias, d_attended, logit_scale):
    def one_row(d_bias, row_args):
        heads_row, mask_row, d_row = row_args
        att_probs = row_probs(heads_row, mask_row, tri_bias, logit_scale)
        d_probs = jnp.einsum('jhd,khd->hjk', d_row, heads_row[:, 2], preferred_element_type=jnp.float32)
        d_val = jnp.einsum('hjk,jhd->khd', att_probs.astype(jnp.bfloat16), d_row, preferred_element_type=jnp.float32)
        d_logits = att_probs * (d_probs - jnp.sum(d_probs * att_probs, axis=-1, keepdims=True))
        d_scaled = (d_logits * logit_scale).astype(jnp.bfloat16)
        d_query = jnp.einsum('hjk,khd->jhd', d_scaled, heads_row[:, 1], preferred_element_type=jnp.float32)
        d_key = jnp.einsum('hjk,jhd->khd', d_scaled, heads_row[:, 0], preferred_element_type=jnp.float32)
        return d_bias + d_logits, jnp.stack([d_query, d_key, d_val], axis=1).astype(jnp.bfloat16)
    return lax.scan(one_row, jnp.zeros(tri_bias.shape, jnp.float32), (qkvg, mask_bias, d_attended))


def block_fwd(pair_in, mask_bias, weights, collect_bias):
    ln_gain, ln_bias, w_proj, w_bias, b_gate, w_out, b_out = weights
    row_count, col_count = pair_in.shape[0], pair_in.shape[1]
    head_count = w_bias.shape[-1]
    attn_width = b_gate.shape[-1]
    head_dim = attn_width // head_count
    normed, x_hat, inv_std = layer_norm(pair_in, ln_gain, ln_bias)
    projected = jnp.einsum('rnc,ce->rne', normed, w_proj, preferred_element_type=jnp.float32).astype(jnp.bfloat16)
    qkvg = projected.reshape(row_count, col_count, 4, head_count, head_dim)
    own_bias = jnp.einsum('rnc,ch->hrn', normed, w_bias, preferred_element_type=jnp.float32).astype(jnp.bfloat16)
    tri_bias = collect_bias(own_bias)
    attended = attend(qkvg, mask_bias, tri_bias, head_dim ** -0.5).reshape(row_count, col_count, attn_width)
    gate_val = jax.nn.sigmoid(projected[:, :, 3 * attn_width:].astype(jnp.float32) + b_gate)
    gated_out = (attended * gate_val).astype(jnp.bfloat16)
    block_out = pair_in.astype(jnp.float32) + jnp.einsum('rne,ec->rnc', gated_out, w_out, preferred_element_type=jnp.float32) + b_out
    saved_fwd = (normed, x_hat, inv_std, qkvg, tri_bias, attended, gate_val, gated_out)
    return block_out.astype(jnp.bfloat16), saved_fwd


def block_bwd(d_block, mask_bias, weights, saved_fwd, spread_bias):
    ln_gain = weights[0]
    w_proj = weights[2]
    w_bias = weights[3]
    w_out = weights[5]
    normed, x_hat, inv_std, qkvg, tri_bias, attended, gate_val, gated_out = saved_fwd
    row_count, col_count, attn_width = gated_out.shape
    head_count = w_bias.shape[-1]
    head_dim = attn_width // head_count
    d_wide = d_block.astype(jnp.float32)
    d_low = d_block.astype(jnp.bfloat16)
    b_out_grad = jnp.sum(d_wide, axis=(0, 1))
    w_out_grad = jnp.einsum('rne,rnc->ec', gated_out, d_low, preferred_element_type=jnp.float32)
    d_gated = jnp.einsum('rnc,ec->rne', d_low, w_out, preferred_element_type=jnp.float32)
    d_gate_lin = d_gated * attended * gate_val * (1.0 - gate_val)
    b_gate_grad = jnp.sum(d_gate_lin, axis=(0, 1))
    d_attended = (d_gated * gate_val).astype(jnp.bfloat16).reshape(row_count, col_count, head_count, head_dim)
    d_bias_all, d_qkv = attend_bwd(qkvg, mask_bias, tri_bias, d_attended, head_dim ** -0.5)
    d_bias_own = spread_bias(d_bias_all).astype(jnp.bfloat16)
    d_gate_heads = d_gate_lin.astype(jnp.bfloat16).reshape(row_count, col_count, 1, head_count, head_dim)
    d_proj = jnp.concatenate([d_qkv, d_gate_heads], axis=2).reshape(row_count, col_count, 4 * attn_width)
    d_normed = jnp.einsum('rne,ce->rnc', d_proj, w_proj, preferred_element_type=jnp.float32) + jnp.einsum('hrn,ch->rnc', d_bias_own, w_bias, preferred_element_type=jnp.float32)
    w_proj_grad = jnp.einsum('rnc,rne->ce', normed, d_proj, preferred_element_type=jnp.float32)
    w_bias_grad = jnp.einsum('rnc,hrn->ch', normed, d_bias_own, preferred_element_type=jnp.float32)
    d_in, gain_grad, shift_grad = layer_norm_bwd(d_normed, x_hat, inv_std, ln_gain)
    return d_wide + d_in, (gain_grad, shift_grad, w_proj_grad, w_bias_grad, b_gate_grad, w_out_grad, b_out_grad)


def solution(mesh):
    row_spec = P(('dp', 'dap'), None, None)
    mask_spec = P(('dp', 'dap'), None)
    grad_spec = P('dp')

    def gather_bias(own_bias):
        return lax.all_gather(own_bias, 'dap', axis=1, tiled=True)

    def scatter_bias(d_bias_all):
        return lax.psum_scatter(d_bias_all, 'dap', scatter_dimension=1, tiled=True)

    def to_columns(row_split):
        return lax.all_to_all(jnp.swapaxes(row_split, 0, 1), 'dap', 0, 1, tiled=True)

    def per_device(z, pair_mask, dz_out, ln_scale, ln_shift, w_proj, w_bias, b_gate, w_out, b_out):
        stacked = (ln_scale, ln_shift, w_proj, w_bias, b_gate, w_out, b_out)
        start_w = tuple(arr[0] for arr in stacked)
        end_w = tuple(arr[1] for arr in stacked)
        mask_rows = (pair_mask.astype(jnp.float32) - 1.0) * MASK_FILL
        mask_cols = (to_columns(pair_mask).astype(jnp.float32) - 1.0) * MASK_FILL
        mid_rows, saved_start = block_fwd(z, mask_rows, start_w, gather_bias)
        mid_cols = to_columns(mid_rows)
        out_cols, saved_end = block_fwd(mid_cols, mask_cols, end_w, gather_bias)
        z_out = to_columns(out_cols)
        d_out_cols = to_columns(dz_out)
        d_mid_cols, grads_end = block_bwd(d_out_cols, mask_cols, end_w, saved_end, scatter_bias)
        d_mid = to_columns(d_mid_cols.astype(jnp.bfloat16))
        d_z, grads_start = block_bwd(d_mid, mask_rows, start_w, saved_start, scatter_bias)
        weight_grads = tuple(lax.psum(jnp.stack([g_start, g_end]), 'dap') for g_start, g_end in zip(grads_start, grads_end))
        return (z_out, d_z.astype(jnp.bfloat16)) + weight_grads

    return jax.shard_map(per_device, mesh=mesh, in_specs=(row_spec, mask_spec, row_spec) + (P(),) * 7, out_specs=(row_spec, row_spec) + (grad_spec,) * 7, check_vma=False)
```

profile of v0, /device:TPU:21, one launch (start us, length us, event | category | flops | bytes accessed | tf_op | source)
XLA Modules:
  0.0 533.6 jit_solution(7675343570069661239)
XLA Ops:
  8.7 10.7 %all-to-all-start.1 = ((s32[16,8,8]{1,2,0:T(8,128)}), s32[16,8,8]{1,2,0:T(8,128)}, u32[]{:S(2)}, u32[]{:S(2)}) async-start(s32[16,8,8]{1,2,0:T(8,128)} %copy.291), calls=%async_computation.1 | async-start | bytes 131072 | tf_op jit(solution)/shard_map/all_to_all | solution.py:110
  27.2 17.6 %all_gather.6 = bf16[4,128,128]{2,0,1:T(4,128)(2,1)S(1)} all-gather(bf16[4,8,128]{2,0,1:T(4,128)(2,1)S(1)} %fusion.100), channel_id=1, replica_groups=mesh['dp'=4,'dap'=16] {'dap'}, dimensions={1}, use_global_device_ids=true | all-gather | bytes 139264 | tf_op jit(solution)/shard_map/all_gather | solution.py:104
  44.9 6.3 %while.46 = (s32[]{:T(128)}, f32[8,128,4,32]{1,3,2,0:T(8,128)S(1)}, bf16[8,128,4,4,32]{1,4,3,2,0:T(8,128)(2,1)S(1)}, bf16[4,128,128]{1,2,0:T(8,128)(2,1)S(1)}, f32[8,128]{1,0:T(8,128)S(1)}, /*index=5*/s32[]{:T(128)}) while((s32[]{:T(128)}, f32[8,128,4,32]{1,3,2,0:T(8,128)S(1)}, bf16[8,128,4,4,32]{1,4,3,2,0:T(8,128)(2,1)S(1)}, ...), condition=%wide.region_5.6_spmd, body=%wide.region_2.5_spmd.sunk | while | flops 13435648 | bytes 1546321 | solution.py:34
  55.7 4.8 all-to-all-start
  63.5 8.3 %all-to-all-done = bf16[128,8,128]{2,1,0:T(8,128)(2,1)S(1)} async-done(((bf16[128,8,128]{2,1,0:T(8,128)(2,1)}), bf16[128,8,128]{2,1,0:T(8,128)(2,1)S(1)}, u32[]{:S(2)}, u32[]{:S(2)}) %all-to-all-start) | async-done | bytes 262176 | tf_op jit(solution)/shard_map/all_to_all | solution.py:110
  71.8 4.3 all-to-all-start.3
  77.6 17.4 %all_gather.7 = bf16[4,128,128]{2,0,1:T(4,128)(2,1)S(1)} all-gather(bf16[4,8,128]{2,0,1:T(4,128)(2,1)S(1)} %fusion.101), channel_id=1, replica_groups=mesh['dp'=4,'dap'=16] {'dap'}, dimensions={1}, use_global_device_ids=true | all-gather | bytes 139264 | tf_op jit(solution)/shard_map/all_gather | solution.py:104
  99.2 21.3 %while.47 = (s32[]{:T(128)}, f32[8,128,4,32]{1,3,2,0:T(8,128)}, bf16[8,128,4,4,32]{1,4,3,2,0:T(8,128)(2,1)S(1)}, bf16[4,128,128]{1,2,0:T(8,128)(2,1)S(1)}, f32[8,128]{1,0:T(8,128)S(1)}, /*index=5*/s32[]{:T(128)}) while((s32[]{:T(128)}, f32[8,128,4,32]{1,3,2,0:T(8,128)}, bf16[8,128,4,4,32]{1,4,3,2,0:T(8,128)(2,1)S(1)}, ...), condition=%wide.region_11.12_spmd, body=%wide.region_8.11_spmd.sunk | while | flops 13435648 | bytes 1546829 | solution.py:34
  123.5 2.1 copy.294
  127.2 2.9 fusion.168
  132.0 86.5 %while.48 = (s32[]{:T(128)}, f32[4,128,128]{1,2,0:T(8,128)}, bf16[8,128,3,4,32]{1,4,3,2,0:T(8,128)(2,1)}, bf16[8,128,4,4,32]{1,4,3,2,0:T(8,128)(2,1)S(1)}, bf16[...) while((s32[]{:T(128)}, f32[4,128,128]{1,2,0:T(8,128)}, ...), condition=%wide.region_16.17_spmd.clone, body=%wide.region_12.0_spmd.clone.sunk | while | flops 23218176 | bytes 4875403 | solution.py:48
  220.9 45.6 %all-reduce.9 = bf16[4,128,128]{2,0,1:T(4,128)(2,1)S(1)} all-reduce(f32[4,128,128]{2,0,1:T(4,128)S(1)} %copy.308), channel_id=2, replica_groups=mesh['dp'=4,'dap'=16] {'dap'}, use_global_device_ids=true, to_apply=%region_17.18.clone | all-reduce | flops 65536 | bytes 393216
  271.6 9.7 %all-to-all-start.4 = ((bf16[128,8,128]{2,1,0:T(8,128)(2,1)}), bf16[128,8,128]{2,1,0:T(8,128)(2,1)S(1)}, u32[]{:S(2)}, u32[]{:S(2)}) async-start(bf16[128,8,128]{2,1,0:T(8,128)(2,1)} %copy.310), calls=%async_computation.4 | async-start | bytes 524288 | tf_op jit(solution)/shard_map/all_to_all | solution.py:110
  286.9 5.8 %all-to-all-done.4 = bf16[128,8,128]{2,1,0:T(8,128)(2,1)S(1)} async-done(((bf16[128,8,128]{2,1,0:T(8,128)(2,1)}), bf16[128,8,128]{2,1,0:T(8,128)(2,1)S(1)}, u32[]{:S(2)}, u32[]{:S(2)}) %all-to-all-start.4) | async-done | bytes 262176 | tf_op jit(solution)/shard_map/all_to_all | solution.py:110
  292.6 3.7 all-to-all-start.2
  297.3 2.5 fusion.170
  300.2 61.3 %while.49 = (s32[]{:T(128)}, f32[4,128,128]{1,2,0:T(8,128)}, bf16[8,128,3,4,32]{1,4,3,2,0:T(8,128)(2,1)S(1)}, bf16[8,128,4,4,32]{1,4,3,2,0:T(8,128)(2,1)S(1)}, b...) while((s32[]{:T(128)}, f32[4,128,128]{1,2,0:T(8,128)}, ...), condition=%wide.region_24.25_spmd.clone, body=%wide.region_20.24_spmd.clone.sunk | while | flops 23218176 | bytes 4865659 | solution.py:48
  313.5 2.0 select_add_fusion.5
  321.2 2.0 select_add_fusion.5
  328.8 2.0 select_add_fusion.5
  336.5 2.0 select_add_fusion.5
  362.7 46.8 %all-reduce.10 = bf16[4,128,128]{2,0,1:T(4,128)(2,1)S(1)} all-reduce(f32[4,128,128]{2,0,1:T(4,128)S(1)} %copy.320), channel_id=3, replica_groups=mesh['dp'=4,'dap'=16] {'dap'}, use_global_device_ids=true, to_apply=%region_25.26.clone | all-reduce | flops 65536 | bytes 393216
  417.6 27.6 %all-reduce.2 = (f32[2,128]{1,0:T(2,128)}, f32[2,128]{1,0:T(2,128)}, f32[2,128,4]{1,2,0:T(4,128)}, f32[2,128]{1,0:T(2,128)}, f32[2,128]{1,0:T(2,128)}) all-reduce(f32[2,128]{1,0:T(2,128)S(1)} %pad_maximum_fusion.5, f32[2,128]{1,0:T(2,128)S(1)} %pad_maximum_fusion.6, ...), channel_id=1, replica_groups=mesh['dp'=4,'dap'=16] {'dap'}, use_global_device_ids=true, to_apply=%region_30.31 | all-reduce | flops 2048 | bytes 16384 | tf_op jit(solution)/shard_map/psum | solution.py:126
  446.5 77.6 %all-reduce.8.cloned.1.call-done = (f32[2,128,512]{2,1,0:T(8,128)}, f32[2,128,128]{2,1,0:T(8,128)}) async-done(((f32[2,128,512]{2,1,0:T(8,128)}, f32[2,128,128]{2,1,0:T(8,128)}), (f32[2,128,512]{2,1,0:T(8,128)}, f32[2,128,128]{2,1,0:T(8,128)})) %all-reduce.8.cloned.1.call-update) | async-done | bytes 655376 | tf_op jit(solution)/shard_map/psum | solution.py:126
  (430 shorter events, 222.1 us)
Async XLA Ops:
  7.2 17.4 %copy-start = (bf16[8,128,128]{2,1,0:T(8,128)(2,1)S(1)}, bf16[8,128,128]{2,1,0:T(8,128)(2,1)}, u32[]{:S(2)}) copy-start(bf16[8,128,128]{2,1,0:T(8,128)(2,1)} %param.18) | copy-start | bytes 786436
  8.7 47.1 %all-to-all-start.1 = ((s32[16,8,8]{1,2,0:T(8,128)}), s32[16,8,8]{1,2,0:T(8,128)}, u32[]{:S(2)}, u32[]{:S(2)}) async-start(s32[16,8,8]{1,2,0:T(8,128)} %copy.291), calls=%async_computation.1 | async-start | bytes 131072 | tf_op jit(solution)/shard_map/all_to_all | solution.py:110
  23.3 71.8 %copy-start.31 = (f32[128]{0:T(128)}, f32[128]{0:T(128)S(1)}, u32[]{:S(2)}) copy-start(f32[128]{0:T(128)S(1)} %get-tuple-element.416) | copy-start | bytes 1540
  26.0 28.5 %copy-start.1 = (bf16[8,128,512]{2,1,0:T(8,128)(2,1)}, bf16[8,128,512]{2,1,0:T(8,128)(2,1)S(1)}, u32[]{:S(2)}) copy-start(bf16[8,128,512]{2,1,0:T(8,128)(2,1)S(1)} %convolution_convert_fusion.7) | copy-start | bytes 3145732
  55.7 16.1 %all-to-all-start = ((bf16[128,8,128]{2,1,0:T(8,128)(2,1)}), bf16[128,8,128]{2,1,0:T(8,128)(2,1)S(1)}, u32[]{:S(2)}, u32[]{:S(2)}) async-start(bf16[128,8,128]{2,1,0:T(8,128)(2,1)} %copy.281), calls=%async_computation | async-start | bytes 524288 | tf_op jit(solution)/shard_map/all_to_all | solution.py:110
  61.4 15.7 %copy-start.34 = (bf16[2,128,4]{1,2,0:T(4,128)(2,1)S(1)}, bf16[2,128,4]{1,2,0:T(4,128)(2,1)}, u32[]{:S(2)}) copy-start(bf16[2,128,4]{1,2,0:T(4,128)(2,1)} %param.24) | copy-start | bytes 6148
  61.4 15.7 %copy-start.45 = (f32[128]{0:T(128)S(1)}, f32[128]{0:T(128)}, u32[]{:S(2)}) copy-start(f32[128]{0:T(128)} %get-tuple-element.418) | copy-start | bytes 1540
  71.8 53.7 %all-to-all-start.3 = ((bf16[128,8,128]{2,1,0:T(8,128)(2,1)}), bf16[128,8,128]{2,1,0:T(8,128)(2,1)}, u32[]{:S(2)}, u32[]{:S(2)}) async-start(bf16[128,8,128]{2,1,0:T(8,128)(2,1)} %bitcast.359), calls=%async_computation.3 | async-start | bytes 524288 | tf_op jit(solution)/shard_map/all_to_all | solution.py:110
  77.1 18.0 %copy-start.20 = (bf16[2,128,512]{2,1,0:T(8,128)(2,1)S(1)}, bf16[2,128,512]{2,1,0:T(8,128)(2,1)}, u32[]{:S(2)}) copy-start(bf16[2,128,512]{2,1,0:T(8,128)(2,1)} %param.23) | copy-start | bytes 786436
  218.5 47.9 %copy-start.16 = (f32[8,16,8]{2,1,0:T(8,128)S(1)}, f32[8,16,8]{2,1,0:T(8,128)}, u32[]{:S(2)}) copy-start(f32[8,16,8]{2,1,0:T(8,128)} %copy.299) | copy-start | bytes 12292
  218.5 48.0 %copy-start.17 = (f32[8,16,8]{2,1,0:T(8,128)S(1)}, f32[8,16,8]{2,1,0:T(8,128)}, u32[]{:S(2)}) copy-start(f32[8,16,8]{2,1,0:T(8,128)} %copy.309) | copy-start | bytes 12292
  218.5 48.1 %copy-start.2 = (bf16[8,128,3,4,32]{1,4,3,2,0:T(8,128)(2,1)S(1)}, bf16[8,128,3,4,32]{1,4,3,2,0:T(8,128)(2,1)}, u32[]{:S(2)}) copy-start(bf16[8,128,3,4,32]{1,4,3,2,0:T(8,128)(2,1)} %get-tuple-element.141) | copy-start | bytes 2359300
  269.0 12.3 %copy-start.8 = (bf16[8,128,128]{2,1,0:T(8,128)(2,1)S(1)}, bf16[8,128,128]{2,1,0:T(8,128)(2,1)}, u32[]{:S(2)}) copy-start(bf16[8,128,128]{2,1,0:T(8,128)(2,1)} %get-tuple-element.409) | copy-start | bytes 786436
  270.7 12.5 %copy-start.25 = (bf16[2,128,128]{2,1,0:T(8,128)(2,1)S(1)}, bf16[2,128,128]{2,1,0:T(8,128)(2,1)}, u32[]{:S(2)}) copy-start(bf16[2,128,128]{2,1,0:T(8,128)(2,1)} %param.26) | copy-start | bytes 196612
  270.7 12.4 %copy-start.42 = (f32[128]{0:T(128)S(1)}, f32[128]{0:T(128)}, u32[]{:S(2)}) copy-start(f32[128]{0:T(128)} %get-tuple-element.411) | copy-start | bytes 1540
  271.6 21.0 %all-to-all-start.4 = ((bf16[128,8,128]{2,1,0:T(8,128)(2,1)}), bf16[128,8,128]{2,1,0:T(8,128)(2,1)S(1)}, u32[]{:S(2)}, u32[]{:S(2)}) async-start(bf16[128,8,128]{2,1,0:T(8,128)(2,1)} %copy.310), calls=%async_computation.4 | async-start | bytes 524288 | tf_op jit(solution)/shard_map/all_to_all | solution.py:110
  285.3 12.0 %copy-start.4 = (f32[8,128,128]{2,1,0:T(8,128)S(1)}, f32[8,128,128]{2,1,0:T(8,128)}, u32[]{:S(2)}) copy-start(f32[8,128,128]{2,1,0:T(8,128)} %copy-done.3) | copy-start | bytes 1572868
  285.3 12.0 %copy-start.39 = (f32[128]{0:T(128)S(1)}, f32[128]{0:T(128)}, u32[]{:S(2)}) copy-start(f32[128]{0:T(128)} %copy-done.38) | copy-start | bytes 1540
  292.6 122.4 %all-to-all-start.2 = ((bf16[128,8,128]{2,1,0:T(8,128)(2,1)}), bf16[128,8,128]{2,1,0:T(8,128)(2,1)S(1)}, u32[]{:S(2)}, u32[]{:S(2)}) async-start(bf16[128,8,128]{2,1,0:T(8,128)(2,1)} %copy.295), calls=%async_computation.2 | async-start | bytes 524288 | tf_op jit(solution)/shard_map/all_to_all | solution.py:110
  296.3 227.8 %all-reduce.8.cloned.1.call-start = ((), (), s32[]{:S(2)}) async-start(), calls=%async_computation.5 | async-start | bytes 1310720 | tf_op jit(solution)/shard_map/psum | solution.py:126
  300.2 109.3 %copy-start.27 = (f32[128]{0:T(128)S(1)}, f32[128]{0:T(128)}, u32[]{:S(2)}) copy-start(f32[128]{0:T(128)} %copy-done.26) | copy-start | bytes 1540
  300.2 109.3 %copy-start.30 = (f32[128]{0:T(128)S(1)}, f32[128]{0:T(128)}, u32[]{:S(2)}) copy-start(f32[128]{0:T(128)} %copy-done.29) | copy-start | bytes 1540
  361.5 49.0 %copy-start.36 = (bf16[2,128,4]{1,2,0:T(4,128)(2,1)S(1)}, bf16[2,128,4]{1,2,0:T(4,128)(2,1)}, u32[]{:S(2)}) copy-start(bf16[2,128,4]{1,2,0:T(4,128)(2,1)} %param.24) | copy-start | bytes 6148
  361.5 50.1 %copy-start.13 = (bf16[8,128,128]{2,1,0:T(8,128)(2,1)S(1)}, bf16[8,128,128]{2,1,0:T(8,128)(2,1)}, u32[]{:S(2)}) copy-start(bf16[8,128,128]{2,1,0:T(8,128)(2,1)} %get-tuple-element.405) | copy-start | bytes 786436
  (43 other events, 103.0 us)
Sparse Core Ops, SparseCore 0:
  417.5 106.5 all-reduce.7
where the time goes:
time: 538 us; the launch traced here: 534 us
  blocking collectives  155 us (29%)
  matrix products  146 us (27%)
  waiting for transfers between devices  91.7 us (17%)
  other arithmetic  54 us (10%)
  local copies, waits for them, and re-layouts  36.9 us (7%)
  starting transfers between devices  33.2 us (6%)
  between operations  15.5 us (3%)
    unnamed x2, blocking collectives  92.4 us
    psum x1, waiting for transfers between devices, per_device(): lax.psum(jnp.stack([g_start, g_end]), 'dap')  77.6 us
    all_gather x2, blocking collectives, gather_bias(): return lax.all_gather(own_bias, 'dap', axis=1, tiled=True)  34.9 us
    all_to_all x5, starting transfers between devices, to_columns(): lax.all_to_all(jnp.swapaxes(row_split, 0, 1), 'dap', 0, 1, tiled=True)  33.2 us
    sub x16, other arithmetic, one_row(): d_probs - jnp.sum(d_probs * att_probs, axis=-1, keepdims=True)  30.9 us
    sub x32, matrix products, row_probs(): return jax.nn.softmax(logits * logit_scale + tri_bias + mask_row, axis=-1)  30.4 us
    psum x1, blocking collectives, per_device(): lax.psum(jnp.stack([g_start, g_end]), 'dap')  27.6 us
    dot_general x16, matrix products, one_row(): jnp.einsum('hjk,jhd->khd', d_scaled, heads_row[:, 0], preferred_element_t...  25.2 us
  transfers between devices with their start and end apart: 6, of which 3 were waited for; matrix products, arithmetic and copies ran while one was open for 24% of the time, Pallas kernels for 0%

commit v1 on v0

v1 whole, which is shorter than its diff:
```python
import functools

import jax
import jax.numpy as jnp
from jax import lax
from jax.experimental import pallas as pl
from jax.experimental.pallas import tpu as pltpu
from jax.sharding import PartitionSpec as P

EPS = 1e-5
MASK_FILL = 1e9
LOG2E = 1.4426950408889634
F32 = jnp.float32
BF16 = jnp.bfloat16
NN = (((1,), (0,)), ((), ()))
NT = (((1,), (1,)), ((), ()))


def dot(a, b, dims=NN):
    return lax.dot_general(a, b, dims, preferred_element_type=F32)


class Exchange:
    def __init__(self, group, axis, send, recv, send_sem, recv_sem, same=False):
        self.group, self.axis, self.send, self.recv = group, axis, send, recv
        self.send_sem, self.recv_sem, self.same = send_sem, recv_sem, same

    def start(self):
        me = lax.axis_index(self.axis)
        half = self.group // 2
        order = [half]
        for hop in range(half - 1, 0, -2):
            order += [hop, self.group - hop]
        for hop in range(half - 2, 0, -2):
            order += [hop, self.group - hop]
        for hop in order:
            peer = lax.rem(me + hop, self.group)
            pltpu.make_async_remote_copy(
                src_ref=self.send if self.same else self.send.at[peer],
                dst_ref=self.recv.at[me],
                send_sem=self.send_sem,
                recv_sem=self.recv_sem,
                device_id={self.axis: peer},
                device_id_type=pl.DeviceIdType.MESH,
            ).start()
        self.recv[me] = self.send[...] if self.same else self.send[me]

    def _all(self):
        some = self.recv.at[pl.ds(0, self.group - 1)]
        return pltpu.make_async_remote_copy(
            src_ref=some,
            dst_ref=some,
            send_sem=self.send_sem,
            recv_sem=self.recv_sem,
            device_id={self.axis: lax.axis_index(self.axis)},
            device_id_type=pl.DeviceIdType.MESH,
        )

    def wait_recv(self):
        self._all().wait_recv()

    def wait_send(self):
        self._all().wait_send()


def kernel(dims, *refs):
    rows, n, ch, heads, hd, group, axis = dims
    hdim = hd // heads
    scale = hdim ** -0.5
    pairs = rows // 2
    two = 2 * n
    wide = heads * n
    (z_ref, mask_ref, dz_ref, lns_ref, lnb_ref, wp_ref, wb_ref, bg_ref, wo_ref, bo_ref,
     zo_out, zg_out, lns_out, lnb_out, wp_out, wb_out, bg_out, wo_out, bo_out,
     wpt, wot, wbt, wbp, col,
     xt, xh, inv, a_s, qt, kt, vt, kv, g_s, ot, ut, btmp, qbd, dbd, dot_s, dgt, dpt, dnt, pf, bias, db, maskb, stage,
     wacc, small, shard,
     b_send, b_recv, mid_send, mid_recv, dz_send, dz_recv, mk_send, mk_recv, zo_send, zo_recv, dm_send, dm_recv,
     db_send, db_recv, w_send, w_recv, w_part, w_full, sm_send, sm_recv,
     send_sems, recv_sems) = refs
    me = lax.axis_index(axis)

    def exchange(slot, send, recv, same=False):
        return Exchange(group, axis, send, recv, send_sems.at[slot], recv_sems.at[slot], same)

    ex_b = [exchange(s, b_send.at[s], b_recv.at[s], True) for s in range(2)]
    ex_mid = exchange(2, mid_send, mid_recv)
    ex_dz = exchange(3, dz_send, dz_recv)
    ex_mask = exchange(4, mk_send, mk_recv, True)
    ex_zo = exchange(5, zo_send, zo_recv)
    ex_dm = exchange(6, dm_send, dm_recv)
    ex_db = [exchange(7 + s, db_send.at[s], db_recv.at[s]) for s in range(2)]
    ex_w = [exchange(9 + s, w_send.at[s], w_recv.at[s]) for s in range(2)]
    ex_wf = [exchange(11 + s, w_part.at[s], w_full.at[s], True) for s in range(2)]
    ex_small = exchange(13, sm_send, sm_recv, True)

    barrier = pltpu.get_barrier_semaphore()
    for hop in range(1, group):
        pl.semaphore_signal(barrier, inc=1, device_id={axis: lax.rem(me + hop, group)},
                            device_id_type=pl.DeviceIdType.MESH)

    head_pick = (lax.broadcasted_iota(jnp.int32, (16, heads), 0) == lax.broadcasted_iota(jnp.int32, (16, heads), 1)).astype(BF16)
    for s in range(2):
        wpt[s] = wp_ref[s].T
        wot[s] = wo_ref[s].T
        wbt[s] = dot(head_pick, wb_ref[s], NT).astype(BF16)
        wbp[s] = dot(wb_ref[s], head_pick, NT).astype(BF16)
        for place, ref in enumerate((lns_ref, lnb_ref, bg_ref, bo_ref)):
            col[s, place] = jnp.broadcast_to(ref[s:s + 1, :], (n, ch)).T

    def zero_diag(i, carry):
        qbd[i] = jnp.zeros((hd, wide), BF16)
        dbd[i] = jnp.zeros((hd, wide), BF16)
        return carry
    lax.fori_loop(0, rows, zero_diag, 0)

    def column(s, place):
        one = col[s, place]
        return jnp.concatenate([one, one], axis=1)

    def store_diag(ref, t, value):
        for r in range(2):
            for h in range(heads):
                ref[2 * t + r, h * hdim:(h + 1) * hdim, h * n:(h + 1) * n] = value[h * hdim:(h + 1) * hdim, r * n:(r + 1) * n]

    def staged(t):
        return [stage[pl.ds(2 * t + r, n, stride=rows), :] for r in range(2)]

    def unpack(recv):
        stage[...] = recv[...].astype(F32).reshape(group * rows * rows, ch)

    def pack(send, t, value):
        parts = [value[r * n:(r + 1) * n].reshape(group, n // group, ch) for r in range(2)]
        send[:, pl.ds(pl.multiple_of(t * 16, 16), 16), :] = jnp.concatenate(parts, axis=1).astype(BF16)

    def project(s, t, x):
        centred = x - jnp.mean(x, axis=0, keepdims=True)
        inv_std = lax.rsqrt(jnp.mean(centred * centred, axis=0, keepdims=True) + EPS)
        x_hat = centred * inv_std
        a_t = (x_hat * column(s, 0) + column(s, 1)).astype(BF16)
        xt[s, t] = x
        xh[s, t] = x_hat
        inv[s, t] = jnp.broadcast_to(inv_std, (8, two))
        a = a_t.T
        a_s[s, t] = a
        p = dot(wpt[s], a_t).astype(BF16)
        qt[s, t] = p[:hd]
        kt[s, t] = p[hd:2 * hd]
        vt[s, t] = p[2 * hd:3 * hd]
        store_diag(qbd, t, p[:hd])
        g_s[s, t] = jax.nn.sigmoid(p[3 * hd:].astype(F32) + column(s, 2))
        kv[s, t] = dot(a, wp_ref[s, :, hd:3 * hd]).astype(BF16)
        b_t = dot(wbt[s], a_t)
        btmp[pl.ds(pl.multiple_of(t * 32, 32), 32), :] = jnp.concatenate([b_t[:, :n], b_t[:, n:]], axis=0)

    def send_bias(s):
        for h in range(0, heads, 2):
            some = [btmp[pl.ds(h + r, rows, stride=16), :] for r in range(2)]
            b_send[s, h * rows:(h + 2) * rows, :] = jnp.concatenate(some, axis=0).astype(BF16)
        ex_b[s].start()

    def take_bias(s):
        ex_b[s].wait_recv()
        got = b_recv[s].astype(F32).reshape(group, heads, rows, n)
        for h in range(heads):
            bias[:, h * n:(h + 1) * n] = got[:, h].reshape(n, n).T * LOG2E

    def probs(s, t, r):
        i = 2 * t + r
        logits = dot(kv[s, t, r * n:(r + 1) * n, :hd], qbd[i])
        fill = maskb[s, i]
        logits = logits * (scale * LOG2E) + bias[...] + jnp.concatenate([fill] * heads, axis=1)
        e = jnp.exp2(logits - jnp.max(logits, axis=0, keepdims=True))
        return e * (1.0 / jnp.sum(e, axis=0, keepdims=True))

    def attend(s, t, r, p_low):
        v = vt[s, t]
        return jnp.concatenate(
            [dot(v[h * hdim:(h + 1) * hdim, r * n:(r + 1) * n], p_low[:, h * n:(h + 1) * n]) for h in range(heads)], axis=0)

    def block_out(s, t):
        u = ut[s, t]
        y = xt[s, t] + dot(wot[s], u) + column(s, 3)
        return y.T

    def attend_bwd(s, t, r, p, p_low):
        i = 2 * t + r
        d_p = dot(kv[s, t, r * n:(r + 1) * n, hd:], dbd[i])
        d_l = p * (d_p - jnp.sum(d_p * p, axis=0, keepdims=True))
        db[...] += d_l
        d_s = (d_l * scale).astype(BF16)
        at = slice(r * n, (r + 1) * n)
        for h in range(heads):
            hs = slice(h * hdim, (h + 1) * hdim)
            d_sh = d_s[:, h * n:(h + 1) * n]
            d_q = dot(kt[s, t, hs, at], d_sh)
            d_k = dot(qt[s, t, hs, at], d_sh, NT)
            d_v = dot(dot_s[t, hs, at], p_low[:, h * n:(h + 1) * n], NT)
            dpt[t, h * hdim:(h + 1) * hdim, at] = d_q.astype(BF16)
            dpt[t, hd + h * hdim:hd + (h + 1) * hdim, at] = d_k.astype(BF16)
            dpt[t, 2 * hd + h * hdim:2 * hd + (h + 1) * hdim, at] = d_v.astype(BF16)

    def gate_bwd(s, t, b_out_sum):
        d_y = jnp.concatenate(staged(t), axis=0)
        d_low = d_y.astype(BF16)
        d_gated = dot(wo_ref[s], d_low, NT)
        dgt[t] = d_gated
        d_o = (d_gated * g_s[s, t]).astype(BF16)
        dot_s[t] = d_o
        store_diag(dbd, t, d_o)
        return b_out_sum + jnp.sum(d_y, axis=0, keepdims=True)

    def after_attention(s, t, gate_sum):
        g = g_s[s, t]
        d_lin = dgt[t] * ot[s, t] * g * (1.0 - g)
        dpt[t, 3 * hd:, :] = d_lin.astype(BF16)
        dnt[t] = dot(wp_ref[s], dpt[t])
        return gate_sum + d_lin

    def add_weights(s, t):
        wacc[:4 * hd] += dot(dpt[t], a_s[s, t])
        d_low = jnp.concatenate(staged(t), axis=0).astype(BF16)
        wacc[4 * hd:] += dot(ut[s, t], d_low)

    def send_weights(s):
        top = wacc[:4 * hd].reshape(group, 4 * hd // group, ch)
        low = wacc[4 * hd:].reshape(group, hd // group, ch)
        w_send[s] = jnp.concatenate([top, low], axis=1).astype(BF16)
        ex_w[s].start()

    def send_bias_grad(s):
        for h in range(0, heads, 2):
            some = [db[:, (h + r) * n:(h + r + 1) * n].T.reshape(group, rows, n) for r in range(2)]
            db_send[s, :, h * rows:(h + 2) * rows, :] = jnp.concatenate(some, axis=1).astype(BF16)
        ex_db[s].start()

    def take_bias_grad(s):
        ex_db[s].wait_recv()
        return jnp.sum(db_recv[s].astype(F32), axis=0).astype(BF16)

    def norm_bwd(s, t, d_own, sums):
        at16 = lax.broadcasted_iota(jnp.int32, (16, heads * rows), 0)
        at32 = lax.broadcasted_iota(jnp.int32, (16, heads * rows), 1)
        rows_of = [dot((at32 == at16 * rows + (2 * t + r)).astype(BF16), d_own) for r in range(2)]
        d_b = jnp.concatenate(rows_of, axis=1).astype(BF16)
        d_n = dnt[t] + dot(wbp[s], d_b)
        x_hat = xh[s, t]
        d_hat = d_n * column(s, 0)
        along = jnp.mean(d_hat * x_hat, axis=0, keepdims=True)
        d_in = inv[s, t, 0:1, :] * (d_hat - jnp.mean(d_hat, axis=0, keepdims=True) - x_hat * along)
        gain_sum, shift_sum, wb_sum = sums
        d_x = d_in.T + jnp.concatenate(staged(t), axis=0)
        return d_x, (gain_sum + d_n * x_hat, shift_sum + d_n, wb_sum + dot(d_b, a_s[s, t]))

    def lanes_to_row(value):
        return jnp.sum((value[:, :n] + value[:, n:]).T, axis=0, keepdims=True)

    def store_small(s, sums, gate_sum, b_out_sum):
        gain_sum, shift_sum, wb_sum = sums
        small[8 * s:8 * s + 1, :] = lanes_to_row(gain_sum)
        small[8 * s + 1:8 * s + 2, :] = lanes_to_row(shift_sum)
        small[8 * s + 2:8 * s + 3, :] = lanes_to_row(gate_sum)
        small[8 * s + 3:8 * s + 4, :] = b_out_sum
        small[8 * s + 4:8 * s + 8, :] = wb_sum[:heads]

    zero_row = jnp.zeros((1, ch), F32)
    zero_tile = jnp.zeros((ch, two), F32)
    zero_sums = (zero_tile, zero_tile, jnp.zeros((16, ch), F32))

    def project_rows(t, carry):
        project(0, t, jnp.concatenate([z_ref[2 * t + r].astype(F32).T for r in range(2)], axis=1))
        return carry
    lax.fori_loop(0, pairs, project_rows, 0)
    pl.semaphore_wait(barrier, group - 1)
    send_bias(0)

    def pack_dz(t, carry):
        pack(dz_send, t, jnp.concatenate([dz_ref[2 * t + r].astype(F32) for r in range(2)], axis=0))
        return carry
    lax.fori_loop(0, pairs, pack_dz, 0)
    fill_rows = (mask_ref[...].astype(F32) - 1.0) * (MASK_FILL * LOG2E)
    for i in range(rows):
        maskb[0, i] = jnp.broadcast_to(fill_rows[i:i + 1, :], (n, n)).T
    mk_send[...] = jnp.concatenate([mask_ref[...].astype(F32)] * 2, axis=0).astype(BF16)
    take_bias(0)
    ex_dz.start()
    ex_mask.start()

    def forward_rows(t, carry):
        for r in range(2):
            p = probs(0, t, r)
            pf[2 * t + r] = p
            ot[0, t, :, r * n:(r + 1) * n] = attend(0, t, r, p.astype(BF16))
        ut[0, t] = (ot[0, t] * g_s[0, t]).astype(BF16)
        pack(mid_send, t, block_out(0, t))
        return carry
    lax.fori_loop(0, pairs, forward_rows, 0)
    ex_mid.start()

    ex_mid.wait_recv()
    unpack(mid_recv)

    def project_cols(t, carry):
        project(1, t, jnp.concatenate([x.T for x in staged(t)], axis=1))
        return carry
    lax.fori_loop(0, pairs, project_cols, 0)
    send_bias(1)

    ex_dz.wait_recv()
    unpack(dz_recv)
    ex_mask.wait_recv()
    whole = mk_recv[...].astype(F32).reshape(group, 2, rows, n)[:, 0].reshape(n, n).astype(BF16)
    for i in range(rows):
        pick = (lax.broadcasted_iota(jnp.int32, (n, n), 0) == me * rows + i).astype(BF16)
        maskb[1, i] = (dot(whole, pick) - 1.0) * (MASK_FILL * LOG2E)
    b_out_sum = lax.fori_loop(0, pairs, lambda t, acc: gate_bwd(1, t, acc), zero_row)
    db[...] = jnp.zeros((n, wide), F32)
    take_bias(1)

    def both_rows(t, carry):
        for r in range(2):
            p = probs(1, t, r)
            p_low = p.astype(BF16)
            ot[1, t, :, r * n:(r + 1) * n] = attend(1, t, r, p_low)
            attend_bwd(1, t, r, p, p_low)
        return carry
    lax.fori_loop(0, pairs, both_rows, 0)
    send_bias_grad(1)

    wacc[...] = jnp.zeros(wacc.shape, F32)

    def finish_cols(t, gate_sum):
        ut[1, t] = (ot[1, t] * g_s[1, t]).astype(BF16)
        pack(zo_send, t, block_out(1, t))
        gate_sum = after_attention(1, t, gate_sum)
        add_weights(1, t)
        return gate_sum
    gate_sum = lax.fori_loop(0, pairs, finish_cols, zero_tile)
    d_own = take_bias_grad(1)

    def norm_cols(t, sums):
        d_x, sums = norm_bwd(1, t, d_own, sums)
        pack(dm_send, t, d_x)
        return sums
    sums = lax.fori_loop(0, pairs, norm_cols, zero_sums)
    ex_dm.start()
    ex_zo.start()
    send_weights(1)
    store_small(1, sums, gate_sum, b_out_sum)

    db[...] = jnp.zeros((n, wide), F32)
    wacc[...] = jnp.zeros(wacc.shape, F32)
    ex_dm.wait_recv()
    unpack(dm_recv)
    b_out_sum = lax.fori_loop(0, pairs, lambda t, acc: gate_bwd(0, t, acc), zero_row)

    def backward_rows(t, carry):
        for r in range(2):
            p = pf[2 * t + r]
            attend_bwd(0, t, r, p, p.astype(BF16))
        return carry
    lax.fori_loop(0, pairs, backward_rows, 0)
    send_bias_grad(0)

    def finish_rows(t, gate_sum):
        gate_sum = after_attention(0, t, gate_sum)
        add_weights(0, t)
        return gate_sum
    gate_sum = lax.fori_loop(0, pairs, finish_rows, zero_tile)
    send_weights(0)
    d_own = take_bias_grad(0)

    def norm_rows(t, sums):
        d_x, sums = norm_bwd(0, t, d_own, sums)
        for r in range(2):
            zg_out[2 * t + r] = d_x[r * n:(r + 1) * n].astype(BF16)
        return sums
    sums = lax.fori_loop(0, pairs, norm_rows, zero_sums)
    store_small(0, sums, gate_sum, b_out_sum)
    sm_send[...] = small[...]
    ex_small.start()

    def reduce_weights(s):
        ex_w[s].wait_recv()
        shard[...] = jnp.sum(w_recv[s].astype(F32), axis=0)
        w_part[s] = shard[...].astype(BF16)
        ex_wf[s].start()
    reduce_weights(1)
    reduce_weights(0)

    ex_zo.wait_recv()
    unpack(zo_recv)

    def store_out(t, carry):
        for r, value in enumerate(staged(t)):
            zo_out[2 * t + r] = value.astype(BF16)
        return carry
    lax.fori_loop(0, pairs, store_out, 0)

    def store_weights(s):
        ex_wf[s].wait_recv()
        full = w_full[s].astype(F32)
        cut = 4 * hd // group
        wp_out[s] = full[:, :cut].reshape(4 * hd, ch).T
        wo_out[s] = full[:, cut:].reshape(hd, ch)
    store_weights(1)

    ex_small.wait_recv()
    total = jnp.sum(sm_recv[...], axis=0)
    for s in range(2):
        for place, ref in enumerate((lns_out, lnb_out, bg_out, bo_out)):
            ref[s:s + 1, :] = total[8 * s + place:8 * s + place + 1, :]
    small[...] = total
    turned = jnp.concatenate([small[...]] * (n // 16), axis=0).T
    for s in range(2):
        wb_out[s] = turned[:, 8 * s + 4:8 * s + 4 + heads]
    store_weights(0)

    for one in ex_b + [ex_mid, ex_dz, ex_mask, ex_zo, ex_dm] + ex_db + ex_w + ex_wf + [ex_small]:
        one.wait_send()


def solution(mesh):
    axis = 'dap'
    group = mesh.shape[axis]
    row_spec = P(('dp', axis), None, None)
    mask_spec = P(('dp', axis), None)
    grad_spec = P('dp')

    def per_device(z, pair_mask, dz_out, ln_scale, ln_shift, w_proj, w_bias, b_gate, w_out, b_out):
        rows, n, ch = z.shape
        heads = w_bias.shape[-1]
        hd = b_gate.shape[-1]
        pairs, two, wide = rows // 2, 2 * n, heads * n
        piece = (group, rows * rows, ch)
        w_rows = 5 * hd // group

        def vmem(shape, dtype):
            return pltpu.VMEM(shape, dtype)

        like = [z, z, ln_scale, ln_shift, w_proj, w_bias, b_gate, w_out, b_out]
        out_shape = [jax.ShapeDtypeStruct(a.shape, BF16 if k < 2 else F32) for k, a in enumerate(like)]
        scratch = [
            vmem((2, 4 * hd, ch), BF16), vmem((2, ch, hd), BF16), vmem((2, 16, ch), BF16), vmem((2, ch, 16), BF16), vmem((2, 4, ch, n), F32),
            vmem((2, pairs, ch, two), F32), vmem((2, pairs, ch, two), F32), vmem((2, pairs, 8, two), F32), vmem((2, pairs, two, ch), BF16),
            vmem((2, pairs, hd, two), BF16), vmem((2, pairs, hd, two), BF16), vmem((2, pairs, hd, two), BF16), vmem((2, pairs, two, 2 * hd), BF16),
            vmem((2, pairs, hd, two), F32), vmem((2, pairs, hd, two), F32), vmem((2, pairs, hd, two), BF16), vmem((rows * 16, n), F32),
            vmem((rows, hd, wide), BF16), vmem((rows, hd, wide), BF16), vmem((pairs, hd, two), BF16), vmem((pairs, hd, two), F32),
            vmem((pairs, 4 * hd, two), BF16), vmem((pairs, ch, two), F32), vmem((rows, n, wide), F32), vmem((n, wide), F32), vmem((n, wide), F32),
            vmem((2, rows, n, n), F32), vmem((group * rows * rows, ch), F32),
            vmem((5 * hd, ch), F32), vmem((16, ch), F32), vmem((w_rows, ch), F32),
            vmem((2, heads * rows, n), BF16), vmem((2, group, heads * rows, n), BF16), vmem(piece, BF16), vmem(piece, BF16), vmem(piece, BF16), vmem(piece, BF16),
            vmem((2 * rows, n), BF16), vmem((group, 2 * rows, n), BF16), vmem(piece, BF16), vmem(piece, BF16), vmem(piece, BF16), vmem(piece, BF16),
            vmem((2, group, heads * rows, n), BF16), vmem((2, group, heads * rows, n), BF16),
            vmem((2, group, w_rows, ch), BF16), vmem((2, group, w_rows, ch), BF16), vmem((2, w_rows, ch), BF16), vmem((2, group, w_rows, ch), BF16),
            vmem((16, ch), F32), vmem((group, 16, ch), F32),
            pltpu.SemaphoreType.DMA((14,)), pltpu.SemaphoreType.DMA((14,)),
        ]
        return pl.pallas_call(
            functools.partial(kernel, (rows, n, ch, heads, hd, group, axis)),
            out_shape=out_shape,
            in_specs=[pl.BlockSpec(memory_space=pltpu.VMEM)] * 10,
            out_specs=[pl.BlockSpec(memory_space=pltpu.VMEM)] * 9,
            scratch_shapes=scratch,
            compiler_params=pltpu.CompilerParams(collective_id=0, has_side_effects=True, vmem_limit_bytes=60 * 1024 * 1024),
        )(z, pair_mask, dz_out, ln_scale, ln_shift, w_proj, w_bias, b_gate, w_out, b_out)

    return jax.shard_map(per_device, mesh=mesh, in_specs=(row_spec, mask_spec, row_spec) + (P(),) * 7,
                         out_specs=(row_spec, row_spec) + (grad_spec,) * 7, check_vma=False)
```

time: 538 us -> 97.8 us (0.18)
  blocking collectives: 155 us -> 0 us
  matrix products: 146 us -> 0 us
  waiting for transfers between devices: 91.7 us -> 0 us
  Pallas kernels: 0 us -> 87.7 us
  other arithmetic: 54 us -> 0 us
  starting transfers between devices: 33.2 us -> 0 us
  local copies, waits for them, and re-layouts: 36.9 us -> 9.31 us
  between operations: 15.5 us -> 0.67 us
    dot_general x114 -> x0, matrix products: 116 us -> none  [the longest x16 25.2 us: one_row(): jnp.einsum('hjk,jhd->khd', d_scaled, heads_row[:, 0], preferred_element_t...]
    unnamed x2 -> x0, blocking collectives: 92.4 us -> none
    pallas_call x0 -> x1, Pallas kernels: none -> 87.7 us  [per_device(): pl.pallas_call(functools.partial(kernel, (rows, n, ch, heads, hd, group,...]
    psum x1 -> x0, waiting for transfers between devices: 77.6 us -> none  [per_device(): lax.psum(jnp.stack([g_start, g_end]), 'dap')]
    all_gather x2 -> x0, blocking collectives: 34.9 us -> none  [gather_bias(): return lax.all_gather(own_bias, 'dap', axis=1, tiled=True)]
    all_to_all x5 -> x0, starting transfers between devices: 33.2 us -> none  [to_columns(): lax.all_to_all(jnp.swapaxes(row_split, 0, 1), 'dap', 0, 1, tiled=True)]
    sub x16 -> x0, other arithmetic: 30.9 us -> none  [one_row(): d_probs - jnp.sum(d_probs * att_probs, axis=-1, keepdims=True)]
    sub x32 -> x0, matrix products: 30.4 us -> none  [row_probs(): return jax.nn.softmax(logits * logit_scale + tri_bias + mask_row, axis=-1)]
  transfers between devices with their start and end apart: 6 -> 0, of which waited for: 3 -> 0; matrix products, arithmetic and copies ran while one was open for 24% -> 0% of each run, Pallas kernels for 0% -> 0%
where the time goes in v1:
time: 97.8 us; the launch traced here: 97.6 us
  Pallas kernels  87.7 us (90%)
  local copies, waits for them, and re-layouts  9.31 us (10%)
    pallas_call x1, Pallas kernels, per_device(): pl.pallas_call(functools.partial(kernel, (rows, n, ch, heads, hd, group,...  87.7 us
    unnamed x23, local copies, waits for them, and re-layouts  7.69 us

profile of v1, /device:TPU:21, one launch (start us, length us, event | category | flops | bytes accessed | tf_op | source)
XLA Modules:
  0.0 97.6 jit_solution(12742411199883565186)
XLA Ops:
  0.6 1.4 %copy.19.refs_6_ = bf16[2,128,4]{2,1,0:T(8,128)(2,1)} copy(bf16[2,128,4]{1,2,0:T(4,128)(2,1)} %param.16) | data formatting | bytes 4096 | tf_op args[6]
  2.1 87.7 %shard_map.169 = (bf16[8,128,128]{2,1,0:T(8,128)(2,1)}, bf16[8,128,128]{2,1,0:T(8,128)(2,1)}, f32[2,128]{1,0:T(2,128)}, f32[2,128]{1,0:T(2,128)}, f32[2,128,512]...) custom-call(bf16[8,128,128]{2,1,0:T(8,128)(2,1)} %refs_0_.1, ...), custom_call_target="tpu_custom_call" | custom-call | tf_op jit(solution)/shard_map/pallas_call | solution.py:459
  89.7 0.0 copy-start.1
  89.7 1.6 %copy.20 = f32[2,128,4]{1,2,0:T(4,128)} copy(f32[2,128,4]{2,1,0:T(8,128)} %get-tuple-element.14) | data formatting | bytes 8192 | tf_op jit(solution)/shard_map/pallas_call | solution.py:459
  91.4 1.7 %copy.29 = bf16[8,128,128]{2,1,0:T(8,128)(2,1)} copy(bf16[8,128,128]{2,1,0:T(8,128)(2,1)} %get-tuple-element.27) | data formatting | bytes 524288
  93.1 0.0 copy-done.1
  93.1 0.0 copy-start.6
  93.1 0.7 copy.30
  93.8 0.0 copy-done.6
  93.8 0.0 copy-start.5
  93.8 0.6 copy.31
  94.4 0.1 copy-done.5
  94.5 0.6 copy.32
  95.0 0.0 copy-done
  95.0 0.0 copy-start.4
  95.0 0.0 copy-start.2
  95.0 0.8 copy.33
  95.8 0.0 copy-done.4
  95.8 0.6 copy.34
  96.4 0.0 copy-done.2
  96.4 0.0 copy-start.3
  96.4 0.7 copy.35
  97.1 0.0 copy-done.3
  97.1 0.6 copy.36
  (1 shorter events, 0.0 us)
Async XLA Ops:
  89.7 3.4 %copy-start.1 = (bf16[8,128,128]{2,1,0:T(8,128)(2,1)S(1)}, bf16[8,128,128]{2,1,0:T(8,128)(2,1)}, u32[]{:S(2)}) copy-start(bf16[8,128,128]{2,1,0:T(8,128)(2,1)} %get-tuple-element.28) | copy-start | bytes 786436
  91.4 3.7 %copy-start = (f32[2,128,512]{2,1,0:T(8,128)S(1)}, f32[2,128,512]{2,1,0:T(8,128)}, u32[]{:S(2)}) copy-start(f32[2,128,512]{2,1,0:T(8,128)} %get-tuple-element.31) | copy-start | bytes 1572868
  93.1 0.7 copy-start.6
  93.8 0.7 copy-start.5
  95.0 0.8 copy-start.4
  95.0 1.4 %copy-start.2 = (f32[2,128,128]{2,1,0:T(8,128)S(1)}, f32[2,128,128]{2,1,0:T(8,128)}, u32[]{:S(2)}) copy-start(f32[2,128,128]{2,1,0:T(8,128)} %get-tuple-element.34) | copy-start | bytes 393220
  96.4 0.7 copy-start.3

commit v2 on v1

--- a/solution.py
+++ b/solution.py
@@ -70,15 +70,21 @@
     pairs = rows // 2
     two = 2 * n
     wide = heads * n
-    (z_ref, mask_ref, dz_ref, lns_ref, lnb_ref, wp_ref, wb_ref, bg_ref, wo_ref, bo_ref,
-     zo_out, zg_out, lns_out, lnb_out, wp_out, wb_out, bg_out, wo_out, bo_out,
+    operands = refs[:10]
+    local = refs[-11:-1]
+    (z_ref, mask_ref, dz_ref, lns_ref, lnb_ref, wp_ref, wb_ref, bg_ref, wo_ref, bo_ref) = local
+    load_sems, refs = refs[-1], refs[10:-11]
+    (zo_recv, zg_out, w_full, sm_recv,
      wpt, wot, wbt, wbp, col,
      xt, xh, inv, a_s, qt, kt, vt, kv, g_s, ot, ut, btmp, qbd, dbd, dot_s, dgt, dpt, dnt, pf, bias, db, maskb, stage,
      wacc, small, shard,
-     b_send, b_recv, mid_send, mid_recv, dz_send, dz_recv, mk_send, mk_recv, zo_send, zo_recv, dm_send, dm_recv,
-     db_send, db_recv, w_send, w_recv, w_part, w_full, sm_send, sm_recv,
+     b_send, b_recv, mid_send, mid_recv, dz_send, dz_recv, mk_send, mk_recv, zo_send, dm_send, dm_recv,
+     db_send, db_recv, w_send, w_recv, w_part, sm_send,
      send_sems, recv_sems) = refs
     me = lax.axis_index(axis)
+    loads = [pltpu.make_async_copy(src, dst, load_sems.at[k]) for k, (src, dst) in enumerate(zip(operands, local))]
+    for one in loads:
+        one.start()
 
     def exchange(slot, send, recv, same=False):
         return Exchange(group, axis, send, recv, send_sems.at[slot], recv_sems.at[slot], same)
@@ -99,12 +105,16 @@
         pl.semaphore_signal(barrier, inc=1, device_id={axis: lax.rem(me + hop, group)},
                             device_id_type=pl.DeviceIdType.MESH)
 
+    for k in (3, 4, 5, 6, 7, 8, 9):
+        loads[k].wait()
     head_pick = (lax.broadcasted_iota(jnp.int32, (16, heads), 0) == lax.broadcasted_iota(jnp.int32, (16, heads), 1)).astype(BF16)
+    eye = (lax.broadcasted_iota(jnp.int32, (ch, ch), 0) == lax.broadcasted_iota(jnp.int32, (ch, ch), 1)).astype(BF16)
     for s in range(2):
         wpt[s] = wp_ref[s].T
         wot[s] = wo_ref[s].T
-        wbt[s] = dot(head_pick, wb_ref[s], NT).astype(BF16)
-        wbp[s] = dot(wb_ref[s], head_pick, NT).astype(BF16)
+        w_heads = dot(head_pick, wb_ref[s]).astype(BF16)
+        wbt[s] = w_heads
+        wbp[s] = dot(eye, w_heads, NT).astype(BF16)
         for place, ref in enumerate((lns_ref, lnb_ref, bg_ref, bo_ref)):
             col[s, place] = jnp.broadcast_to(ref[s:s + 1, :], (n, ch)).T
 
@@ -267,12 +277,17 @@
     zero_tile = jnp.zeros((ch, two), F32)
     zero_sums = (zero_tile, zero_tile, jnp.zeros((16, ch), F32))
 
+    loads[0].wait()
+
     def project_rows(t, carry):
         project(0, t, jnp.concatenate([z_ref[2 * t + r].astype(F32).T for r in range(2)], axis=1))
         return carry
     lax.fori_loop(0, pairs, project_rows, 0)
     pl.semaphore_wait(barrier, group - 1)
     send_bias(0)
+
+    loads[1].wait()
+    loads[2].wait()
 
     def pack_dz(t, carry):
         pack(dz_send, t, jnp.concatenate([dz_ref[2 * t + r].astype(F32) for r in range(2)], axis=0))
@@ -388,36 +403,29 @@
     reduce_weights(1)
     reduce_weights(0)
 
-    ex_zo.wait_recv()
-    unpack(zo_recv)
-
-    def store_out(t, carry):
-        for r, value in enumerate(staged(t)):
-            zo_out[2 * t + r] = value.astype(BF16)
-        return carry
-    lax.fori_loop(0, pairs, store_out, 0)
-
-    def store_weights(s):
-        ex_wf[s].wait_recv()
-        full = w_full[s].astype(F32)
-        cut = 4 * hd // group
+    for one in [ex_zo, ex_small] + ex_wf:
+        one.wait_recv()
+    for one in ex_b + [ex_mid, ex_dz, ex_mask, ex_zo, ex_dm] + ex_db + ex_w + ex_wf + [ex_small]:
+        one.wait_send()
+
+
+def finish(dims, zo_ref, zg_ref, w_ref, sm_ref,
+           zo_out, zg_out, lns_out, lnb_out, wp_out, wb_out, bg_out, wo_out, bo_out, stage):
+    rows, n, ch, heads, hd, group = dims
+    zg_out[...] = zg_ref[...]
+    stage[...] = zo_ref[...].astype(F32).reshape(group * rows * rows, ch)
+    for i in range(rows):
+        zo_out[i] = stage[pl.ds(i, n, stride=rows), :].astype(BF16)
+    cut = 4 * hd // group
+    for s in range(2):
+        full = w_ref[s].astype(F32)
         wp_out[s] = full[:, :cut].reshape(4 * hd, ch).T
         wo_out[s] = full[:, cut:].reshape(hd, ch)
-    store_weights(1)
-
-    ex_small.wait_recv()
-    total = jnp.sum(sm_recv[...], axis=0)
+    total = jnp.sum(sm_ref[...], axis=0)
     for s in range(2):
         for place, ref in enumerate((lns_out, lnb_out, bg_out, bo_out)):
             ref[s:s + 1, :] = total[8 * s + place:8 * s + place + 1, :]
-    small[...] = total
-    turned = jnp.concatenate([small[...]] * (n // 16), axis=0).T
-    for s in range(2):
-        wb_out[s] = turned[:, 8 * s + 4:8 * s + 4 + heads]
-    store_weights(0)
-
-    for one in ex_b + [ex_mid, ex_dz, ex_mask, ex_zo, ex_dm] + ex_db + ex_w + ex_wf + [ex_small]:
-        one.wait_send()
+        wb_out[s] = total[8 * s + 4:8 * s + 4 + heads]
 
 
 def solution(mesh):
@@ -438,8 +446,11 @@
         def vmem(shape, dtype):
             return pltpu.VMEM(shape, dtype)
 
-        like = [z, z, ln_scale, ln_shift, w_proj, w_bias, b_gate, w_out, b_out]
+        w_heads = jnp.swapaxes(w_bias, 1, 2)
+        like = [z, z, ln_scale, ln_shift, w_proj, w_heads, b_gate, w_out, b_out]
         out_shape = [jax.ShapeDtypeStruct(a.shape, BF16 if k < 2 else F32) for k, a in enumerate(like)]
+        mid_shape = [jax.ShapeDtypeStruct(piece, BF16), jax.ShapeDtypeStruct(z.shape, BF16),
+                     jax.ShapeDtypeStruct((2, group, w_rows, ch), BF16), jax.ShapeDtypeStruct((group, 16, ch), F32)]
         scratch = [
             vmem((2, 4 * hd, ch), BF16), vmem((2, ch, hd), BF16), vmem((2, 16, ch), BF16), vmem((2, ch, 16), BF16), vmem((2, 4, ch, n), F32),
             vmem((2, pairs, ch, two), F32), vmem((2, pairs, ch, two), F32), vmem((2, pairs, 8, two), F32), vmem((2, pairs, two, ch), BF16),
@@ -450,20 +461,31 @@
             vmem((2, rows, n, n), F32), vmem((group * rows * rows, ch), F32),
             vmem((5 * hd, ch), F32), vmem((16, ch), F32), vmem((w_rows, ch), F32),
             vmem((2, heads * rows, n), BF16), vmem((2, group, heads * rows, n), BF16), vmem(piece, BF16), vmem(piece, BF16), vmem(piece, BF16), vmem(piece, BF16),
-            vmem((2 * rows, n), BF16), vmem((group, 2 * rows, n), BF16), vmem(piece, BF16), vmem(piece, BF16), vmem(piece, BF16), vmem(piece, BF16),
+            vmem((2 * rows, n), BF16), vmem((group, 2 * rows, n), BF16), vmem(piece, BF16), vmem(piece, BF16), vmem(piece, BF16),
             vmem((2, group, heads * rows, n), BF16), vmem((2, group, heads * rows, n), BF16),
-            vmem((2, group, w_rows, ch), BF16), vmem((2, group, w_rows, ch), BF16), vmem((2, w_rows, ch), BF16), vmem((2, group, w_rows, ch), BF16),
-            vmem((16, ch), F32), vmem((group, 16, ch), F32),
+            vmem((2, group, w_rows, ch), BF16), vmem((2, group, w_rows, ch), BF16), vmem((2, w_rows, ch), BF16), vmem((16, ch), F32),
             pltpu.SemaphoreType.DMA((14,)), pltpu.SemaphoreType.DMA((14,)),
         ]
-        return pl.pallas_call(
+        operands = (z, pair_mask, dz_out, ln_scale, ln_shift, w_proj, w_heads, b_gate, w_out, b_out)
+        scratch += [vmem(a.shape, a.dtype) for a in operands] + [pltpu.SemaphoreType.DMA((10,))]
+        in_vmem = pl.BlockSpec(memory_space=pltpu.VMEM)
+        mid = pl.pallas_call(
             functools.partial(kernel, (rows, n, ch, heads, hd, group, axis)),
+            out_shape=mid_shape,
+            in_specs=[pl.BlockSpec(memory_space=pltpu.HBM)] * 10,
+            out_specs=[in_vmem] * 4,
+            scratch_shapes=scratch,
+            compiler_params=pltpu.CompilerParams(collective_id=0, has_side_effects=True, vmem_limit_bytes=40 * 1024 * 1024),
+        )(*[pltpu.with_memory_space_constraint(a, pltpu.HBM) for a in operands])
+        out = pl.pallas_call(
+            functools.partial(finish, (rows, n, ch, heads, hd, group)),
             out_shape=out_shape,
-            in_specs=[pl.BlockSpec(memory_space=pltpu.VMEM)] * 10,
-            out_specs=[pl.BlockSpec(memory_space=pltpu.VMEM)] * 9,
-            scratch_shapes=scratch,
-            compiler_params=pltpu.CompilerParams(collective_id=0, has_side_effects=True, vmem_limit_bytes=60 * 1024 * 1024),
-        )(z, pair_mask, dz_out, ln_scale, ln_shift, w_proj, w_bias, b_gate, w_out, b_out)
+            in_specs=[in_vmem] * 4,
+            out_specs=[in_vmem] * 9,
+            scratch_shapes=[vmem((group * rows * rows, ch), F32)],
+            compiler_params=pltpu.CompilerParams(vmem_limit_bytes=16 * 1024 * 1024),
+        )(*mid)
+        return tuple(out[:5]) + (jnp.swapaxes(out[5], 1, 2),) + tuple(out[6:])
 
     return jax.shard_map(per_device, mesh=mesh, in_specs=(row_spec, mask_spec, row_spec) + (P(),) * 7,
                          out_specs=(row_spec, row_spec) + (grad_spec,) * 7, check_vma=False)

time: 97.8 us -> 88.5 us (0.905)
  the two profiles are of different devices: /device:TPU:21 before, /device:TPU:28 now
where the time goes in v2:
time: 88.5 us; the launch traced here: 88.4 us
  Pallas kernels  87.7 us (99%)
    pallas_call x1, Pallas kernels, per_device(): pl.pallas_call(functools.partial(kernel, (rows, n, ch, heads, hd, group,...  86.6 us

profile of v2, /device:TPU:28, one launch (start us, length us, event | category | flops | bytes accessed | tf_op | source)
XLA Modules:
  0.0 88.4 jit_solution(10978900178537984947)
XLA Ops:
  0.6 86.6 %shard_map.169 = (bf16[16,64,128]{2,1,0:T(8,128)(2,1)S(1)}, bf16[8,128,128]{2,1,0:T(8,128)(2,1)S(1)}, bf16[2,16,40,128]{3,2,1,0:T(8,128)(2,1)S(1)}, f32[16,16,128]{2,1,0:T(8,128)S(1)}) custom-call(bf16[8,128,128]{2,1,0:T(8,128)(2,1)} %refs_0_.1, s32[8,128]{1,0:T(8,128)} %refs_1_.1, bf16[8,128,128]{2,1,0:T(8,128)(2,1)} %refs_2_.1, f32[2,128]{1,0:T(2,128)} %refs_3_.1, ...), custom_call_target="tpu_custom_call" | custom-call | tf_op jit(solution)/shard_map/pallas_call | solution.py:472
  87.3 1.1 %shard_map.170 = (bf16[8,128,128]{2,1,0:T(8,128)(2,1)}, bf16[8,128,128]{2,1,0:T(8,128)(2,1)}, f32[2,128]{1,0:T(2,128)}, f32[2,128]{1,0:T(2,128)}, f32[2,128,512]...) custom-call(bf16[16,64,128]{2,1,0:T(8,128)(2,1)S(1)} %get-tuple-element.22, ...), custom_call_target="tpu_custom_call" | custom-call | tf_op jit(solution)/shard_map/pallas_call | solution.py:480

commit v3 on v2

v3 whole, which is shorter than its diff:
```python
import functools

import jax
import jax.numpy as jnp
from jax import lax
from jax.experimental import pallas as pl
from jax.experimental.pallas import tpu as pltpu
from jax.sharding import PartitionSpec as P

EPS = 1e-5
MASK_FILL = 1e9
LOG2E = 1.4426950408889634
F32 = jnp.float32
BF16 = jnp.bfloat16
NN = (((1,), (0,)), ((), ()))
NT = (((1,), (1,)), ((), ()))


def dot(a, b, dims=NN):
    return lax.dot_general(a, b, dims, preferred_element_type=F32)


class Exchange:
    def __init__(self, group, axis, send, recv, send_sem, recv_sem, same=False):
        self.group, self.axis, self.send, self.recv = group, axis, send, recv
        self.send_sem, self.recv_sem, self.same = send_sem, recv_sem, same

    def start(self, part=None):
        me = lax.axis_index(self.axis)
        half = self.group // 2
        order = [half]
        for hop in range(half - 1, 0, -1):
            order += [hop, self.group - hop]
        for hop in order:
            peer = lax.rem(me + hop, self.group)
            source = self.send if self.same else self.send.at[peer] if part is None else self.send.at[peer, part]
            pltpu.make_async_remote_copy(
                src_ref=source,
                dst_ref=self.recv.at[me] if part is None else self.recv.at[me, part],
                send_sem=self.send_sem,
                recv_sem=self.recv_sem,
                device_id={self.axis: peer},
                device_id_type=pl.DeviceIdType.MESH,
            ).start()
        if part is None:
            self.recv[me] = self.send[...] if self.same else self.send[me]
        else:
            self.recv[me, part] = self.send[me, part]

    def _all(self):
        some = self.recv.at[pl.ds(0, self.group - 1)]
        return pltpu.make_async_remote_copy(
            src_ref=some,
            dst_ref=some,
            send_sem=self.send_sem,
            recv_sem=self.recv_sem,
            device_id={self.axis: lax.axis_index(self.axis)},
            device_id_type=pl.DeviceIdType.MESH,
        )

    def wait_recv(self):
        self._all().wait_recv()

    def wait_send(self):
        self._all().wait_send()


class ChipExchange:
    def __init__(self, chips, axis, send, recv, send_sem, recv_sem, same=False):
        self.chips, self.axis, self.send, self.recv = chips, axis, send, recv
        self.send_sem, self.recv_sem, self.same = send_sem, recv_sem, same

    def start(self):
        me = lax.axis_index(self.axis)
        chip, core = me // 2, me % 2
        order = [self.chips // 2]
        for hop in range(self.chips // 2 - 1, 0, -1):
            order += [hop, self.chips - hop]
        for hop in order:
            to = lax.rem(chip + hop, self.chips)
            pltpu.make_async_remote_copy(
                src_ref=self.send if self.same else self.send.at[to],
                dst_ref=self.recv.at[chip],
                send_sem=self.send_sem,
                recv_sem=self.recv_sem,
                device_id={self.axis: 2 * to + core},
                device_id_type=pl.DeviceIdType.MESH,
            ).start()
        self.recv[chip] = self.send[...] if self.same else self.send[chip]

    def _all(self):
        some = self.recv.at[pl.ds(0, self.chips - 1)]
        return pltpu.make_async_remote_copy(
            src_ref=some,
            dst_ref=some,
            send_sem=self.send_sem,
            recv_sem=self.recv_sem,
            device_id={self.axis: lax.axis_index(self.axis)},
            device_id_type=pl.DeviceIdType.MESH,
        )

    def wait_recv(self):
        self._all().wait_recv()

    def wait_send(self):
        self._all().wait_send()


def kernel(dims, *refs):
    rows, n, ch, heads, hd, group, axis = dims
    hdim = hd // heads
    scale = hdim ** -0.5
    pairs = rows // 2
    two = 2 * n
    wide = heads * n
    chips = group // 2
    operands = refs[:10]
    local = refs[-11:-1]
    (z_ref, mask_ref, dz_ref, lns_ref, lnb_ref, wp_ref, wb_ref, bg_ref, wo_ref, bo_ref) = local
    load_sems, refs = refs[-1], refs[10:-11]
    (zo_recv, zg_out, w_full, sm_recv,
     wpt, wot, wbt, wbp, col,
     xt, xh, inv, a_s, at1, qt, kt, vt, kv, g_s, ot, ut, btmp, qbd, dbd, dot_s, dgt, dpt, dnt, dzt, dmt, dlp, dlt, pf, bias, db, maskb, stage,
     wacc,
     b_send, b_recv, mid_send, mid_recv, dz_send, dz_recv, mk_send, mk_recv, zo_send, dm_send, dm_recv,
     db_send, db_recv, w_send, w_half, w_mid, w_recv, w_part, sm_send,
     send_sems, recv_sems) = refs
    me = lax.axis_index(axis)
    core = me % 2
    loads = [pltpu.make_async_copy(src, dst, load_sems.at[k]) for k, (src, dst) in enumerate(zip(operands, local))]
    for one in loads:
        one.start()

    def exchange(slot, send, recv, same=False):
        return Exchange(group, axis, send, recv, send_sems.at[slot], recv_sems.at[slot], same)

    def chip_exchange(slot, send, recv, same=False):
        return ChipExchange(chips, axis, send, recv, send_sems.at[slot], recv_sems.at[slot], same)

    def to_sibling(slot, send, recv):
        return pltpu.make_async_remote_copy(src_ref=send, dst_ref=recv, send_sem=send_sems.at[slot], recv_sem=recv_sems.at[slot],
                                            device_id={axis: me + 1 - 2 * core}, device_id_type=pl.DeviceIdType.MESH)

    ex_b = [exchange(s, b_send.at[s], b_recv.at[s], True) for s in range(2)]
    ex_mid = exchange(2, mid_send, mid_recv)
    ex_dz = exchange(3, dz_send, dz_recv)
    ex_mask = exchange(4, mk_send, mk_recv, True)
    ex_zo = exchange(5, zo_send, zo_recv)
    ex_dm = exchange(6, dm_send, dm_recv)
    ex_db = [exchange(7 + s, db_send.at[s], db_recv.at[s]) for s in range(2)]
    ex_small = [exchange(9 + s, sm_send.at[s], sm_recv.at[s], True) for s in range(2)]
    near_w = [to_sibling(11 + s, w_send.at[s, 1 - core], w_half.at[s]) for s in range(2)]
    ex_w = [chip_exchange(13 + s, w_mid.at[s], w_recv.at[s]) for s in range(2)]
    ex_wf = [chip_exchange(15 + s, w_part.at[s], w_full.at[s, core], True) for s in range(2)]
    near_wf = [to_sibling(17 + s, w_full.at[s, core], w_full.at[s, core]) for s in range(2)]

    barrier = pltpu.get_barrier_semaphore()
    for hop in range(1, group):
        pl.semaphore_signal(barrier, inc=1, device_id={axis: lax.rem(me + hop, group)},
                            device_id_type=pl.DeviceIdType.MESH)

    for k in (3, 4, 5, 6, 7, 8, 9):
        loads[k].wait()
    head_pick = (lax.broadcasted_iota(jnp.int32, (16, heads), 0) == lax.broadcasted_iota(jnp.int32, (16, heads), 1)).astype(BF16)
    eye = (lax.broadcasted_iota(jnp.int32, (ch, ch), 0) == lax.broadcasted_iota(jnp.int32, (ch, ch), 1)).astype(BF16)
    for s in range(2):
        wpt[s] = wp_ref[s].T
        wot[s] = wo_ref[s].T
        w_heads = dot(head_pick, wb_ref[s]).astype(BF16)
        wbt[s] = w_heads
        wbp[s] = dot(eye, w_heads, NT).astype(BF16)
        for place, ref in enumerate((lns_ref, lnb_ref, bg_ref, bo_ref)):
            col[s, place] = jnp.broadcast_to(ref[s:s + 1, :], (n, ch)).T

    def zero_diag(i, carry):
        qbd[i] = jnp.zeros((hd, wide), BF16)
        dbd[i] = jnp.zeros((hd, wide), BF16)
        return carry
    lax.fori_loop(0, rows, zero_diag, 0)

    def column(s, place):
        one = col[s, place]
        return jnp.concatenate([one, one], axis=1)

    def store_diag(ref, t, value):
        for r in range(2):
            for h in range(heads):
                ref[2 * t + r, h * hdim:(h + 1) * hdim, h * n:(h + 1) * n] = value[h * hdim:(h + 1) * hdim, r * n:(r + 1) * n]

    def staged(t):
        return jnp.concatenate([stage[pl.ds(2 * t + r, n, stride=rows), :] for r in range(2)], axis=0)

    def unpack(recv):
        stage[...] = recv[...].astype(F32).reshape(group * rows * rows, ch)

    def pack(send, t, value):
        parts = [value[r * n:(r + 1) * n].reshape(group, n // group, ch) for r in range(2)]
        send[:, pl.ds(pl.multiple_of(t * 16, 16), 16), :] = jnp.concatenate(parts, axis=1).astype(BF16)

    def halves(body, init, ex):
        carry = init
        for k in range(2):
            carry = lax.fori_loop(k * pairs // 2, (k + 1) * pairs // 2, body, carry)
            ex.start(pl.ds(k * rows * rows // 2, rows * rows // 2))
        return carry

    def normalize(s, t, x):
        centred = x - jnp.mean(x, axis=0, keepdims=True)
        inv_std = lax.rsqrt(jnp.mean(centred * centred, axis=0, keepdims=True) + EPS)
        x_hat = centred * inv_std
        return (x_hat * column(s, 0) + column(s, 1)).astype(BF16), x_hat, inv_std

    def keep_norm(s, t, x):
        a_t, x_hat, inv_std = normalize(s, t, x)
        xh[s, t] = x_hat
        inv[s, t] = jnp.broadcast_to(inv_std, (8, two))
        b_t = dot(wbt[s], a_t)
        btmp[pl.ds(pl.multiple_of(t * 32, 32), 32), :] = jnp.concatenate([b_t[:, :n], b_t[:, n:]], axis=0)
        return a_t

    def project(s, t, x, a_t):
        xt[s, t] = x
        a = a_t.T
        a_s[s, t] = a
        p = dot(wpt[s], a_t).astype(BF16)
        qt[s, t] = p[:hd]
        kt[s, t] = p[hd:2 * hd]
        vt[s, t] = p[2 * hd:3 * hd]
        store_diag(qbd, t, p[:hd])
        g = jax.nn.sigmoid(p[3 * hd:].astype(F32) + column(s, 2))
        g_s[s, t] = g
        kv[s, t] = dot(a, wp_ref[s, :, hd:3 * hd]).astype(BF16)
        return g

    def send_bias(s):
        for h in range(0, heads, 2):
            some = [btmp[pl.ds(h + r, rows, stride=16), :] for r in range(2)]
            b_send[s, h * rows:(h + 2) * rows, :] = jnp.concatenate(some, axis=0).astype(BF16)
        ex_b[s].start()

    def take_bias(s):
        ex_b[s].wait_recv()
        got = b_recv[s].astype(F32).reshape(group, heads, rows, n)
        for h in range(heads):
            one = got[:, h].reshape(n, n)
            bias[:, h * n:(h + 1) * n] = (one.T if s == 0 else one) * LOG2E

    def probs(s, t, r):
        i = 2 * t + r
        logits = dot(kv[s, t, r * n:(r + 1) * n, :hd], qbd[i])
        fill = maskb[s, i]
        logits = logits * (scale * LOG2E) + bias[...] + jnp.concatenate([fill] * heads, axis=1)
        e = jnp.exp2(logits - jnp.max(logits, axis=0, keepdims=True))
        return e * (1.0 / jnp.sum(e, axis=0, keepdims=True))

    def attend(s, t):
        for r in range(2):
            p = probs(s, t, r)
            pf[s, 2 * t + r] = p
            p_low = p.astype(BF16)
            v = vt[s, t]
            ot[s, t, :, r * n:(r + 1) * n] = jnp.concatenate(
                [dot(v[h * hdim:(h + 1) * hdim, r * n:(r + 1) * n], p_low[:, h * n:(h + 1) * n]) for h in range(heads)], axis=0)
        u = (ot[s, t] * g_s[s, t]).astype(BF16)
        ut[s, t] = u
        return xt[s, t] + dot(wot[s], u) + column(s, 3)

    def attend_bwd(s, t):
        for r in range(2):
            i = 2 * t + r
            p = pf[s, i]
            p_low = p.astype(BF16)
            d_p = dot(kv[s, t, r * n:(r + 1) * n, hd:], dbd[i])
            d_l = p * (d_p - jnp.sum(d_p * p, axis=0, keepdims=True))
            db[...] += d_l
            d_s = (d_l * scale).astype(BF16)
            at = slice(r * n, (r + 1) * n)
            for h in range(heads):
                hs = slice(h * hdim, (h + 1) * hdim)
                d_sh = d_s[:, h * n:(h + 1) * n]
                d_q = dot(kt[s, t, hs, at], d_sh)
                d_k = dot(qt[s, t, hs, at], d_sh, NT)
                d_v = dot(dot_s[t, hs, at], p_low[:, h * n:(h + 1) * n], NT)
                dpt[t, h * hdim:(h + 1) * hdim, at] = d_q.astype(BF16)
                dpt[t, hd + h * hdim:hd + (h + 1) * hdim, at] = d_k.astype(BF16)
                dpt[t, 2 * hd + h * hdim:2 * hd + (h + 1) * hdim, at] = d_v.astype(BF16)

    def store_d_o(t, d_o):
        dot_s[t] = d_o
        store_diag(dbd, t, d_o)

    def after_attention(s, t, gate_sum):
        g = g_s[s, t]
        d_lin = dgt[t] * ot[s, t] * g * (1.0 - g)
        dpt[t, 3 * hd:, :] = d_lin.astype(BF16)
        return dot(wp_ref[s], dpt[t]), gate_sum + d_lin

    def send_weights(s):
        top = wacc[:4 * hd].reshape(2, chips, 4 * hd // group, ch)
        low = wacc[4 * hd:].reshape(2, chips, hd // group, ch)
        w_send[s] = jnp.concatenate([top, low], axis=2).astype(BF16)
        near_w[s].start()

    def chip_sum_weights(s):
        near_w[s].wait_recv()
        w_mid[s] = (w_send[s, core].astype(F32) + w_half[s].astype(F32)).astype(BF16)
        ex_w[s].start()

    def reduce_weights(s):
        ex_w[s].wait_recv()
        w_part[s] = jnp.sum(w_recv[s].astype(F32), axis=0).astype(BF16)
        ex_wf[s].start()

    def forward_weights(s):
        ex_wf[s].wait_recv()
        near_wf[s].start()

    def send_bias_grad(s):
        for h in range(0, heads, 2):
            some = [db[:, (h + r) * n:(h + r + 1) * n] for r in range(2)]
            some = [(one.T if s == 0 else one).reshape(group, rows, n) for one in some]
            db_send[s, :, h * rows:(h + 2) * rows, :] = jnp.concatenate(some, axis=1).astype(BF16)
        ex_db[s].start()

    def take_bias_grad(s):
        ex_db[s].wait_recv()
        return jnp.sum(db_recv[s].astype(F32), axis=0).astype(BF16)

    def norm_bwd(s, t, d_n, d_own, sums):
        at16 = lax.broadcasted_iota(jnp.int32, (16, heads * rows), 0)
        at32 = lax.broadcasted_iota(jnp.int32, (16, heads * rows), 1)
        rows_of = [dot((at32 == at16 * rows + (2 * t + r)).astype(BF16), d_own) for r in range(2)]
        d_b = jnp.concatenate(rows_of, axis=1).astype(BF16)
        d_n = d_n + dot(wbp[s], d_b)
        x_hat = xh[s, t]
        d_hat = d_n * column(s, 0)
        along = jnp.mean(d_hat * x_hat, axis=0, keepdims=True)
        d_in = inv[s, t, 0:1, :] * (d_hat - jnp.mean(d_hat, axis=0, keepdims=True) - x_hat * along)
        gain_sum, shift_sum, wb_sum = sums
        more = dot(d_b, a_s[0, t]) if s == 0 else dot(d_b, at1[t], NT)
        return d_in, (gain_sum + d_n * x_hat, shift_sum + d_n, wb_sum + more)

    def lanes_to_row(value):
        return jnp.sum((value[:, :n] + value[:, n:]).T, axis=0, keepdims=True)

    def send_small(s, sums, gate_sum, b_out_row):
        gain_sum, shift_sum, wb_sum = sums
        sm_send[s, 0:1, :] = lanes_to_row(gain_sum)
        sm_send[s, 1:2, :] = lanes_to_row(shift_sum)
        sm_send[s, 2:3, :] = lanes_to_row(gate_sum)
        sm_send[s, 3:4, :] = b_out_row
        sm_send[s, 4:4 + heads, :] = wb_sum[:heads]
        ex_small[s].start()

    zero_row = jnp.zeros((1, ch), F32)
    zero_tile = jnp.zeros((ch, two), F32)
    zero_sums = (zero_tile, zero_tile, jnp.zeros((16, ch), F32))

    loads[0].wait()

    def project_rows(t, carry):
        x = jnp.concatenate([z_ref[2 * t + r].astype(F32).T for r in range(2)], axis=1)
        project(0, t, x, keep_norm(0, t, x))
        return carry
    lax.fori_loop(0, pairs, project_rows, 0)
    pl.semaphore_wait(barrier, group - 1)
    send_bias(0)
    loads[1].wait()
    loads[2].wait()

    def pack_dz(t, b_out_row):
        d_y = jnp.concatenate([dz_ref[2 * t + r].astype(F32) for r in range(2)], axis=0)
        pack(dz_send, t, d_y)
        dzt[t] = d_y.T
        return b_out_row + jnp.sum(d_y, axis=0, keepdims=True)
    b_out_row1 = lax.fori_loop(0, pairs, pack_dz, zero_row)
    mk_send[...] = mask_ref[...].astype(F32).astype(BF16)
    ex_dz.start()
    ex_mask.start()
    fill_rows = (mask_ref[...].astype(F32) - 1.0) * (MASK_FILL * LOG2E)
    for i in range(rows):
        maskb[0, i] = jnp.broadcast_to(fill_rows[i:i + 1, :], (n, n)).T
    take_bias(0)

    def forward_rows(t, carry):
        y = attend(0, t)
        pack(mid_send, t, y.T)
        at1[t] = keep_norm(1, t, y.astype(BF16).astype(F32))
        return carry
    halves(forward_rows, 0, ex_mid)
    send_bias(1)

    ex_dz.wait_recv()
    unpack(dz_recv)

    def gate_cols(t, carry):
        d_low = staged(t).astype(BF16)
        dlp[t] = d_low
        dgt[t] = dot(wo_ref[1], d_low, NT)
        return carry
    lax.fori_loop(0, pairs, gate_cols, 0)
    ex_mask.wait_recv()
    whole = mk_recv[...].astype(F32).reshape(n, n).astype(BF16)
    for i in range(rows):
        pick = (lax.broadcasted_iota(jnp.int32, (n, n), 0) == me * rows + i).astype(BF16)
        maskb[1, i] = (dot(whole, pick) - 1.0) * (MASK_FILL * LOG2E)

    ex_mid.wait_recv()
    unpack(mid_recv)

    def project_cols(t, carry):
        x = staged(t).T
        g = project(1, t, x, normalize(1, t, x)[0])
        store_d_o(t, (dgt[t] * g).astype(BF16))
        return carry
    lax.fori_loop(0, pairs, project_cols, 0)
    db[...] = jnp.zeros((n, wide), F32)
    take_bias(1)

    def forward_cols(t, carry):
        pack(zo_send, t, attend(1, t).T)
        return carry
    lax.fori_loop(0, pairs, forward_cols, 0)
    ex_zo.start()

    def backward_cols(t, carry):
        attend_bwd(1, t)
        return carry
    lax.fori_loop(0, pairs, backward_cols, 0)
    send_bias_grad(1)

    def finish_cols(t, gate_sum):
        d_n, gate_sum = after_attention(1, t, gate_sum)
        pack(dm_send, t, d_n.T)
        return gate_sum
    gate_sum1 = halves(finish_cols, zero_tile, ex_dm)

    wacc[...] = jnp.zeros(wacc.shape, F32)

    def weights_cols(t, carry):
        wacc[:4 * hd] += dot(dpt[t], a_s[1, t])
        wacc[4 * hd:] += dot(ut[1, t], dlp[t])
        return carry
    lax.fori_loop(0, pairs, weights_cols, 0)
    send_weights(1)
    db[...] = jnp.zeros((n, wide), F32)
    wacc[...] = jnp.zeros(wacc.shape, F32)
    chip_sum_weights(1)

    ex_dm.wait_recv()
    unpack(dm_recv)
    d_own1 = take_bias_grad(1)

    def norm_and_gate(t, carry):
        sums, b_out_sum = carry
        d_in, sums = norm_bwd(1, t, staged(t).T, d_own1, sums)
        d_y = d_in + dzt[t]
        dmt[t] = d_y
        d_low = d_y.astype(BF16)
        dlt[t] = d_low
        d_gated = dot(wo_ref[0], d_low)
        dgt[t] = d_gated
        store_d_o(t, (d_gated * g_s[0, t]).astype(BF16))
        return sums, b_out_sum + d_y
    sums1, b_out_sum = lax.fori_loop(0, pairs, norm_and_gate, (zero_sums, zero_tile))

    def backward_rows(t, carry):
        attend_bwd(0, t)
        return carry
    lax.fori_loop(0, pairs, backward_rows, 0)
    send_bias_grad(0)

    def finish_rows(t, gate_sum):
        d_n, gate_sum = after_attention(0, t, gate_sum)
        dnt[t] = d_n
        wacc[:4 * hd] += dot(dpt[t], a_s[0, t])
        wacc[4 * hd:] += dot(ut[0, t], dlt[t], NT)
        return gate_sum
    gate_sum0 = lax.fori_loop(0, pairs, finish_rows, zero_tile)
    send_weights(0)
    reduce_weights(1)
    send_small(1, sums1, gate_sum1, b_out_row1)
    b_out_row0 = lanes_to_row(b_out_sum)
    chip_sum_weights(0)
    d_own0 = take_bias_grad(0)

    def norm_rows(t, sums):
        d_in, sums = norm_bwd(0, t, dnt[t], d_own0, sums)
        d_x = (d_in + dmt[t]).T.astype(BF16)
        for r in range(2):
            zg_out[2 * t + r] = d_x[r * n:(r + 1) * n]
        return sums
    sums0 = lax.fori_loop(0, pairs, norm_rows, zero_sums)
    send_small(0, sums0, gate_sum0, b_out_row0)
    reduce_weights(0)
    forward_weights(1)
    forward_weights(0)

    for one in [ex_zo] + ex_small + near_wf:
        one.wait_recv()
    for one in ex_b + [ex_mid, ex_dz, ex_mask, ex_zo, ex_dm] + ex_db + ex_small + near_w + ex_w + ex_wf + near_wf:
        one.wait_send()


def finish(dims, zo_ref, zg_ref, w_ref, sm_ref,
           zo_out, zg_out, lns_out, lnb_out, wp_out, wb_out, bg_out, wo_out, bo_out, stage):
    rows, n, ch, heads, hd, group = dims
    zg_out[...] = zg_ref[...]
    stage[...] = zo_ref[...].astype(F32).reshape(group * rows * rows, ch)
    for i in range(rows):
        zo_out[i] = stage[pl.ds(i, n, stride=rows), :].astype(BF16)
    cut = 4 * hd // group
    for s in range(2):
        full = w_ref[s].astype(F32).reshape(group, 5 * hd // group, ch)
        wp_out[s] = full[:, :cut].reshape(4 * hd, ch).T
        wo_out[s] = full[:, cut:].reshape(hd, ch)
        total = jnp.sum(sm_ref[s], axis=0)
        for place, ref in enumerate((lns_out, lnb_out, bg_out, bo_out)):
            ref[s:s + 1, :] = total[place:place + 1, :]
        wb_out[s] = total[4:4 + heads]


def solution(mesh):
    axis = 'dap'
    group = mesh.shape[axis]
    row_spec = P(('dp', axis), None, None)
    mask_spec = P(('dp', axis), None)
    grad_spec = P('dp')

    def per_device(z, pair_mask, dz_out, ln_scale, ln_shift, w_proj, w_bias, b_gate, w_out, b_out):
        rows, n, ch = z.shape
        heads = w_bias.shape[-1]
        hd = b_gate.shape[-1]
        pairs, two, wide = rows // 2, 2 * n, heads * n
        piece = (group, rows * rows, ch)
        w_rows = 5 * hd // group

        def vmem(shape, dtype):
            return pltpu.VMEM(shape, dtype)

        w_heads = jnp.swapaxes(w_bias, 1, 2)
        like = [z, z, ln_scale, ln_shift, w_proj, w_heads, b_gate, w_out, b_out]
        out_shape = [jax.ShapeDtypeStruct(a.shape, BF16 if k < 2 else F32) for k, a in enumerate(like)]
        chips = group // 2
        mid_shape = [jax.ShapeDtypeStruct(piece, BF16), jax.ShapeDtypeStruct(z.shape, BF16),
                     jax.ShapeDtypeStruct((2, 2, chips, w_rows, ch), BF16), jax.ShapeDtypeStruct((2, group, 8, ch), F32)]
        tile = (pairs, ch, two)
        scratch = [
            vmem((2, 4 * hd, ch), BF16), vmem((2, ch, hd), BF16), vmem((2, 16, ch), BF16), vmem((2, ch, 16), BF16), vmem((2, 4, ch, n), F32),
            vmem((2,) + tile, F32), vmem((2,) + tile, F32), vmem((2, pairs, 8, two), F32), vmem((2, pairs, two, ch), BF16), vmem(tile, BF16),
            vmem((2, pairs, hd, two), BF16), vmem((2, pairs, hd, two), BF16), vmem((2, pairs, hd, two), BF16), vmem((2, pairs, two, 2 * hd), BF16),
            vmem((2, pairs, hd, two), F32), vmem((2, pairs, hd, two), F32), vmem((2, pairs, hd, two), BF16), vmem((rows * 16, n), F32),
            vmem((rows, hd, wide), BF16), vmem((rows, hd, wide), BF16), vmem((pairs, hd, two), BF16), vmem((pairs, hd, two), F32),
            vmem((pairs, 4 * hd, two), BF16), vmem(tile, F32), vmem(tile, F32), vmem(tile, F32), vmem((pairs, two, ch), BF16), vmem(tile, BF16),
            vmem((2, rows, n, wide), F32), vmem((n, wide), F32), vmem((n, wide), F32),
            vmem((2, rows, n, n), F32), vmem((group * rows * rows, ch), F32),
            vmem((5 * hd, ch), F32),
            vmem((2, heads * rows, n), BF16), vmem((2, group, heads * rows, n), BF16), vmem(piece, BF16), vmem(piece, BF16), vmem(piece, BF16), vmem(piece, BF16),
            vmem((rows, n), BF16), vmem((group, rows, n), BF16), vmem(piece, BF16), vmem(piece, BF16), vmem(piece, BF16),
            vmem((2, group, heads * rows, n), BF16), vmem((2, group, heads * rows, n), BF16),
            vmem((2, 2, chips, w_rows, ch), BF16), vmem((2, chips, w_rows, ch), BF16), vmem((2, chips, w_rows, ch), BF16), vmem((2, chips, w_rows, ch), BF16),
            vmem((2, w_rows, ch), BF16), vmem((2, 8, ch), F32),
            pltpu.SemaphoreType.DMA((19,)), pltpu.SemaphoreType.DMA((19,)),
        ]
        operands = (z, pair_mask, dz_out, ln_scale, ln_shift, w_proj, w_heads, b_gate, w_out, b_out)
        scratch += [vmem(a.shape, a.dtype) for a in operands] + [pltpu.SemaphoreType.DMA((10,))]
        in_vmem = pl.BlockSpec(memory_space=pltpu.VMEM)
        mid = pl.pallas_call(
            functools.partial(kernel, (rows, n, ch, heads, hd, group, axis)),
            out_shape=mid_shape,
            in_specs=[pl.BlockSpec(memory_space=pltpu.HBM)] * 10,
            out_specs=[in_vmem] * 4,
            scratch_shapes=scratch,
            compiler_params=pltpu.CompilerParams(collective_id=0, has_side_effects=True, vmem_limit_bytes=40 * 1024 * 1024),
        )(*[pltpu.with_memory_space_constraint(a, pltpu.HBM) for a in operands])
        out = pl.pallas_call(
            functools.partial(finish, (rows, n, ch, heads, hd, group)),
            out_shape=out_shape,
            in_specs=[in_vmem] * 4,
            out_specs=[in_vmem] * 9,
            scratch_shapes=[vmem((group * rows * rows, ch), F32)],
            compiler_params=pltpu.CompilerParams(vmem_limit_bytes=16 * 1024 * 1024),
        )(*mid)
        return tuple(out[:5]) + (jnp.swapaxes(out[5], 1, 2),) + tuple(out[6:])

    return jax.shard_map(per_device, mesh=mesh, in_specs=(row_spec, mask_spec, row_spec) + (P(),) * 7,
                         out_specs=(row_spec, row_spec) + (grad_spec,) * 7, check_vma=False)
```

time: 88.5 us -> 78.8 us (0.89)
  the two profiles are of different devices: /device:TPU:28 before, /device:TPU:21 now
where the time goes in v3:
time: 78.8 us; the launch traced here: 78.7 us
  Pallas kernels  78 us (99%)
    pallas_call x1, Pallas kernels, per_device(): pl.pallas_call(functools.partial(kernel, (rows, n, ch, heads, hd, group,...  76.9 us

profile of v3, /device:TPU:21, one launch (start us, length us, event | category | flops | bytes accessed | tf_op | source)
XLA Modules:
  0.0 78.7 jit_solution(6742309749093898144)
XLA Ops:
  0.6 76.9 %shard_map.169 = (bf16[16,64,128]{2,1,0:T(8,128)(2,1)S(1)}, bf16[8,128,128]{2,1,0:T(8,128)(2,1)S(1)}, bf16[2,2,8,40,128]{4,3,2,1,0:T(8,128)(2,1)S(1)}, f32[2,16,8,128]{3,2,1,0:T(8,128)S(1)}) custom-call(bf16[8,128,128]{2,1,0:T(8,128)(2,1)} %refs_0_.1, s32[8,128]{1,0:T(8,128)} %refs_1_.1, bf16[8,128,128]{2,1,0:T(8,128)(2,1)} %refs_2_.1, f32[2,128]{1,0:T(2,128)} %refs_3_.1, ...), custom_call_target="tpu_custom_call" | custom-call | tf_op jit(solution)/shard_map/pallas_call | solution.py:568
  77.6 1.1 %shard_map.170 = (bf16[8,128,128]{2,1,0:T(8,128)(2,1)}, bf16[8,128,128]{2,1,0:T(8,128)(2,1)}, f32[2,128]{1,0:T(2,128)}, f32[2,128]{1,0:T(2,128)}, f32[2,128,512]...) custom-call(bf16[16,64,128]{2,1,0:T(8,128)(2,1)S(1)} %get-tuple-element.22, ...), custom_call_target="tpu_custom_call" | custom-call | tf_op jit(solution)/shard_map/pallas_call | solution.py:576

commit v4 on v3

--- a/solution.py
+++ b/solution.py
@@ -121,7 +121,7 @@
     (zo_recv, zg_out, w_full, sm_recv,
      wpt, wot, wbt, wbp, col,
      xt, xh, inv, a_s, at1, qt, kt, vt, kv, g_s, ot, ut, btmp, qbd, dbd, dot_s, dgt, dpt, dnt, dzt, dmt, dlp, dlt, pf, bias, db, maskb, stage,
-     wacc,
+     wacc, wsel, dbt,
      b_send, b_recv, mid_send, mid_recv, dz_send, dz_recv, mk_send, mk_recv, zo_send, dm_send, dm_recv,
      db_send, db_recv, w_send, w_half, w_mid, w_recv, w_part, sm_send,
      send_sems, recv_sems) = refs
@@ -197,12 +197,8 @@
         parts = [value[r * n:(r + 1) * n].reshape(group, n // group, ch) for r in range(2)]
         send[:, pl.ds(pl.multiple_of(t * 16, 16), 16), :] = jnp.concatenate(parts, axis=1).astype(BF16)
 
-    def halves(body, init, ex):
-        carry = init
-        for k in range(2):
-            carry = lax.fori_loop(k * pairs // 2, (k + 1) * pairs // 2, body, carry)
-            ex.start(pl.ds(k * rows * rows // 2, rows * rows // 2))
-        return carry
+    def half(k):
+        return pl.ds(k * rows * rows // 2, rows * rows // 2)
 
     def normalize(s, t, x):
         centred = x - jnp.mean(x, axis=0, keepdims=True)
@@ -245,42 +241,53 @@
             one = got[:, h].reshape(n, n)
             bias[:, h * n:(h + 1) * n] = (one.T if s == 0 else one) * LOG2E
 
-    def probs(s, t, r):
-        i = 2 * t + r
-        logits = dot(kv[s, t, r * n:(r + 1) * n, :hd], qbd[i])
-        fill = maskb[s, i]
-        logits = logits * (scale * LOG2E) + bias[...] + jnp.concatenate([fill] * heads, axis=1)
-        e = jnp.exp2(logits - jnp.max(logits, axis=0, keepdims=True))
-        return e * (1.0 / jnp.sum(e, axis=0, keepdims=True))
-
-    def attend(s, t):
-        for r in range(2):
-            p = probs(s, t, r)
-            pf[s, 2 * t + r] = p
-            p_low = p.astype(BF16)
-            v = vt[s, t]
-            ot[s, t, :, r * n:(r + 1) * n] = jnp.concatenate(
-                [dot(v[h * hdim:(h + 1) * hdim, r * n:(r + 1) * n], p_low[:, h * n:(h + 1) * n]) for h in range(heads)], axis=0)
+    def logits(s):
+        for i in range(rows):
+            t, r = divmod(i, 2)
+            fill = maskb[s, i]
+            raw = dot(kv[s, t, r * n:(r + 1) * n, :hd], qbd[i])
+            for h in range(heads):
+                pf[s, i, :, h * n:(h + 1) * n] = raw[:, h * n:(h + 1) * n] * (scale * LOG2E) + fill
+
+    def attend(s, some):
+        for i in some:
+            t, r = divmod(i, 2)
+            for h in range(heads):
+                cols = slice(h * n, (h + 1) * n)
+                x = pf[s, i, :, cols] + bias[:, cols]
+                e = jnp.exp2(x - jnp.max(x, axis=0, keepdims=True))
+                p = e * (1.0 / jnp.sum(e, axis=0, keepdims=True))
+                pf[s, i, :, cols] = p
+                hs = slice(h * hdim, (h + 1) * hdim)
+                ot[s, t, hs, r * n:(r + 1) * n] = dot(vt[s, t, hs, r * n:(r + 1) * n], p.astype(BF16))
+
+    def block_out(s, t):
         u = (ot[s, t] * g_s[s, t]).astype(BF16)
         ut[s, t] = u
         return xt[s, t] + dot(wot[s], u) + column(s, 3)
 
-    def attend_bwd(s, t):
-        for r in range(2):
-            i = 2 * t + r
-            p = pf[s, i]
-            p_low = p.astype(BF16)
-            d_p = dot(kv[s, t, r * n:(r + 1) * n, hd:], dbd[i])
-            d_l = p * (d_p - jnp.sum(d_p * p, axis=0, keepdims=True))
-            db[...] += d_l
-            d_s = (d_l * scale).astype(BF16)
+    def attend_bwd(s, some):
+        def d_probs(i):
+            t, r = divmod(i, 2)
+            return dot(kv[s, t, r * n:(r + 1) * n, hd:], dbd[i])
+        ahead = d_probs(some[0])
+        for k, i in enumerate(some):
+            t, r = divmod(i, 2)
+            d_p = ahead
+            if k + 1 < len(some):
+                ahead = d_probs(some[k + 1])
             at = slice(r * n, (r + 1) * n)
             for h in range(heads):
+                cols = slice(h * n, (h + 1) * n)
+                p = pf[s, i, :, cols]
+                d_ph = d_p[:, cols]
+                d_l = p * (d_ph - jnp.sum(d_ph * p, axis=0, keepdims=True))
+                db[:, cols] += d_l
+                d_s = (d_l * scale).astype(BF16)
                 hs = slice(h * hdim, (h + 1) * hdim)
-                d_sh = d_s[:, h * n:(h + 1) * n]
-                d_q = dot(kt[s, t, hs, at], d_sh)
-                d_k = dot(qt[s, t, hs, at], d_sh, NT)
-                d_v = dot(dot_s[t, hs, at], p_low[:, h * n:(h + 1) * n], NT)
+                d_q = dot(kt[s, t, hs, at], d_s)
+                d_k = dot(qt[s, t, hs, at], d_s, NT)
+                d_v = dot(dot_s[t, hs, at], p.astype(BF16), NT)
                 dpt[t, h * hdim:(h + 1) * hdim, at] = d_q.astype(BF16)
                 dpt[t, hd + h * hdim:hd + (h + 1) * hdim, at] = d_k.astype(BF16)
                 dpt[t, 2 * hd + h * hdim:2 * hd + (h + 1) * hdim, at] = d_v.astype(BF16)
@@ -326,25 +333,33 @@
         ex_db[s].wait_recv()
         return jnp.sum(db_recv[s].astype(F32), axis=0).astype(BF16)
 
-    def norm_bwd(s, t, d_n, d_own, sums):
+    def bias_terms(s, d_own):
+        return [jnp.concatenate([dot(wsel[s, 2 * t + r], d_own) for r in range(2)], axis=1) for t in range(pairs)]
+
+    def head_weight_grad(s, d_own):
         at16 = lax.broadcasted_iota(jnp.int32, (16, heads * rows), 0)
         at32 = lax.broadcasted_iota(jnp.int32, (16, heads * rows), 1)
-        rows_of = [dot((at32 == at16 * rows + (2 * t + r)).astype(BF16), d_own) for r in range(2)]
-        d_b = jnp.concatenate(rows_of, axis=1).astype(BF16)
-        d_n = d_n + dot(wbp[s], d_b)
+        for t in range(pairs):
+            rows_of = [dot((at32 == at16 * rows + (2 * t + r)).astype(BF16), d_own) for r in range(2)]
+            dbt[t] = jnp.concatenate(rows_of, axis=1).astype(BF16)
+        total = None
+        for t in range(pairs):
+            one = dot(dbt[t], a_s[0, t]) if s == 0 else dot(dbt[t], at1[t], NT)
+            total = one if total is None else total + one
+        return total
+
+    def norm_bwd(s, t, d_n, sums):
         x_hat = xh[s, t]
         d_hat = d_n * column(s, 0)
         along = jnp.mean(d_hat * x_hat, axis=0, keepdims=True)
         d_in = inv[s, t, 0:1, :] * (d_hat - jnp.mean(d_hat, axis=0, keepdims=True) - x_hat * along)
-        gain_sum, shift_sum, wb_sum = sums
-        more = dot(d_b, a_s[0, t]) if s == 0 else dot(d_b, at1[t], NT)
-        return d_in, (gain_sum + d_n * x_hat, shift_sum + d_n, wb_sum + more)
+        return d_in, (sums[0] + d_n * x_hat, sums[1] + d_n)
 
     def lanes_to_row(value):
         return jnp.sum((value[:, :n] + value[:, n:]).T, axis=0, keepdims=True)
 
-    def send_small(s, sums, gate_sum, b_out_row):
-        gain_sum, shift_sum, wb_sum = sums
+    def send_small(s, sums, wb_sum, gate_sum, b_out_row):
+        gain_sum, shift_sum = sums
         sm_send[s, 0:1, :] = lanes_to_row(gain_sum)
         sm_send[s, 1:2, :] = lanes_to_row(shift_sum)
         sm_send[s, 2:3, :] = lanes_to_row(gate_sum)
@@ -352,53 +367,55 @@
         sm_send[s, 4:4 + heads, :] = wb_sum[:heads]
         ex_small[s].start()
 
-    zero_row = jnp.zeros((1, ch), F32)
     zero_tile = jnp.zeros((ch, two), F32)
-    zero_sums = (zero_tile, zero_tile, jnp.zeros((16, ch), F32))
+    early, late = range(pairs // 2), range(pairs // 2, pairs)
 
     loads[0].wait()
-
-    def project_rows(t, carry):
+    for t in range(pairs):
         x = jnp.concatenate([z_ref[2 * t + r].astype(F32).T for r in range(2)], axis=1)
         project(0, t, x, keep_norm(0, t, x))
-        return carry
-    lax.fori_loop(0, pairs, project_rows, 0)
     pl.semaphore_wait(barrier, group - 1)
     send_bias(0)
     loads[1].wait()
+    fill_rows = (mask_ref[...].astype(F32) - 1.0) * (MASK_FILL * LOG2E)
+    for i in range(rows):
+        maskb[0, i] = jnp.broadcast_to(fill_rows[i:i + 1, :], (n, n)).T
+    logits(0)
     loads[2].wait()
-
-    def pack_dz(t, b_out_row):
+    b_out_row1 = jnp.zeros((1, ch), F32)
+    for t in range(pairs):
         d_y = jnp.concatenate([dz_ref[2 * t + r].astype(F32) for r in range(2)], axis=0)
         pack(dz_send, t, d_y)
         dzt[t] = d_y.T
-        return b_out_row + jnp.sum(d_y, axis=0, keepdims=True)
-    b_out_row1 = lax.fori_loop(0, pairs, pack_dz, zero_row)
+        b_out_row1 = b_out_row1 + jnp.sum(d_y, axis=0, keepdims=True)
     mk_send[...] = mask_ref[...].astype(F32).astype(BF16)
     ex_dz.start()
     ex_mask.start()
-    fill_rows = (mask_ref[...].astype(F32) - 1.0) * (MASK_FILL * LOG2E)
-    for i in range(rows):
-        maskb[0, i] = jnp.broadcast_to(fill_rows[i:i + 1, :], (n, n)).T
+    at16 = lax.broadcasted_iota(jnp.int32, (16, heads * rows), 0)
+    at32 = lax.broadcasted_iota(jnp.int32, (16, heads * rows), 1)
+    for s in range(2):
+        for i in range(rows):
+            wsel[s, i] = dot(wbp[s], ((at32 == at16 * rows + i) & (at16 < heads)).astype(BF16)).astype(BF16)
     take_bias(0)
 
-    def forward_rows(t, carry):
-        y = attend(0, t)
-        pack(mid_send, t, y.T)
-        at1[t] = keep_norm(1, t, y.astype(BF16).astype(F32))
-        return carry
-    halves(forward_rows, 0, ex_mid)
+    for k, some in enumerate((early, late)):
+        attend(0, range(2 * some[0], 2 * some[-1] + 2))
+        for t in some:
+            y = block_out(0, t)
+            pack(mid_send, t, y.T)
+            xt[1, t] = y.astype(BF16).astype(F32)
+        ex_mid.start(half(k))
+    for t in range(pairs):
+        at1[t] = keep_norm(1, t, xt[1, t])
     send_bias(1)
 
     ex_dz.wait_recv()
     unpack(dz_recv)
-
-    def gate_cols(t, carry):
+    for t in range(pairs):
         d_low = staged(t).astype(BF16)
         dlp[t] = d_low
         dgt[t] = dot(wo_ref[1], d_low, NT)
-        return carry
-    lax.fori_loop(0, pairs, gate_cols, 0)
+    db[...] = jnp.zeros((n, wide), F32)
     ex_mask.wait_recv()
     whole = mk_recv[...].astype(F32).reshape(n, n).astype(BF16)
     for i in range(rows):
@@ -407,53 +424,49 @@
 
     ex_mid.wait_recv()
     unpack(mid_recv)
-
-    def project_cols(t, carry):
+    for t in range(pairs):
         x = staged(t).T
         g = project(1, t, x, normalize(1, t, x)[0])
         store_d_o(t, (dgt[t] * g).astype(BF16))
-        return carry
-    lax.fori_loop(0, pairs, project_cols, 0)
-    db[...] = jnp.zeros((n, wide), F32)
+    logits(1)
     take_bias(1)
-
-    def forward_cols(t, carry):
-        pack(zo_send, t, attend(1, t).T)
-        return carry
-    lax.fori_loop(0, pairs, forward_cols, 0)
+    attend(1, range(rows))
+
+    gate_sum1 = zero_tile
+    for k, some in enumerate((early, late)):
+        attend_bwd(1, range(2 * some[0], 2 * some[-1] + 2))
+        for t in some:
+            d_n, gate_sum1 = after_attention(1, t, gate_sum1)
+            pack(dm_send, t, d_n.T)
+        if k == 1:
+            send_bias_grad(1)
+        ex_dm.start(half(k))
+    for t in range(pairs):
+        pack(zo_send, t, block_out(1, t).T)
     ex_zo.start()
 
-    def backward_cols(t, carry):
-        attend_bwd(1, t)
-        return carry
-    lax.fori_loop(0, pairs, backward_cols, 0)
-    send_bias_grad(1)
-
-    def finish_cols(t, gate_sum):
-        d_n, gate_sum = after_attention(1, t, gate_sum)
-        pack(dm_send, t, d_n.T)
-        return gate_sum
-    gate_sum1 = halves(finish_cols, zero_tile, ex_dm)
-
-    wacc[...] = jnp.zeros(wacc.shape, F32)
-
-    def weights_cols(t, carry):
-        wacc[:4 * hd] += dot(dpt[t], a_s[1, t])
-        wacc[4 * hd:] += dot(ut[1, t], dlp[t])
-        return carry
-    lax.fori_loop(0, pairs, weights_cols, 0)
+    def sum_weights(s):
+        top, low = None, None
+        for t in range(pairs):
+            one = dot(dpt[t], a_s[s, t])
+            two_ = dot(ut[1, t], dlp[t]) if s == 1 else dot(ut[0, t], dlt[t], NT)
+            top, low = (one, two_) if top is None else (top + one, low + two_)
+        wacc[:4 * hd] = top
+        wacc[4 * hd:] = low
+    sum_weights(1)
     send_weights(1)
     db[...] = jnp.zeros((n, wide), F32)
-    wacc[...] = jnp.zeros(wacc.shape, F32)
     chip_sum_weights(1)
 
+    d_own1 = take_bias_grad(1)
+    terms = bias_terms(1, d_own1)
+    for t in range(pairs):
+        dnt[t] = terms[t]
     ex_dm.wait_recv()
     unpack(dm_recv)
-    d_own1 = take_bias_grad(1)
-
-    def norm_and_gate(t, carry):
-        sums, b_out_sum = carry
-        d_in, sums = norm_bwd(1, t, staged(t).T, d_own1, sums)
+    sums1, b_out_sum = (zero_tile, zero_tile), zero_tile
+    for t in range(pairs):
+        d_in, sums1 = norm_bwd(1, t, staged(t).T + dnt[t], sums1)
         d_y = d_in + dzt[t]
         dmt[t] = d_y
         d_low = d_y.astype(BF16)
@@ -461,37 +474,29 @@
         d_gated = dot(wo_ref[0], d_low)
         dgt[t] = d_gated
         store_d_o(t, (d_gated * g_s[0, t]).astype(BF16))
-        return sums, b_out_sum + d_y
-    sums1, b_out_sum = lax.fori_loop(0, pairs, norm_and_gate, (zero_sums, zero_tile))
-
-    def backward_rows(t, carry):
-        attend_bwd(0, t)
-        return carry
-    lax.fori_loop(0, pairs, backward_rows, 0)
+        b_out_sum = b_out_sum + d_y
+
+    attend_bwd(0, range(rows))
     send_bias_grad(0)
-
-    def finish_rows(t, gate_sum):
-        d_n, gate_sum = after_attention(0, t, gate_sum)
-        dnt[t] = d_n
-        wacc[:4 * hd] += dot(dpt[t], a_s[0, t])
-        wacc[4 * hd:] += dot(ut[0, t], dlt[t], NT)
-        return gate_sum
-    gate_sum0 = lax.fori_loop(0, pairs, finish_rows, zero_tile)
+    gate_sum0 = zero_tile
+    for t in range(pairs):
+        dnt[t], gate_sum0 = after_attention(0, t, gate_sum0)
+    sum_weights(0)
     send_weights(0)
     reduce_weights(1)
-    send_small(1, sums1, gate_sum1, b_out_row1)
+    send_small(1, sums1, head_weight_grad(1, d_own1), gate_sum1, b_out_row1)
     b_out_row0 = lanes_to_row(b_out_sum)
     chip_sum_weights(0)
+
     d_own0 = take_bias_grad(0)
-
-    def norm_rows(t, sums):
-        d_in, sums = norm_bwd(0, t, dnt[t], d_own0, sums)
+    terms = bias_terms(0, d_own0)
+    sums0 = (zero_tile, zero_tile)
+    for t in range(pairs):
+        d_in, sums0 = norm_bwd(0, t, dnt[t] + terms[t], sums0)
         d_x = (d_in + dmt[t]).T.astype(BF16)
         for r in range(2):
             zg_out[2 * t + r] = d_x[r * n:(r + 1) * n]
-        return sums
-    sums0 = lax.fori_loop(0, pairs, norm_rows, zero_sums)
-    send_small(0, sums0, gate_sum0, b_out_row0)
+    send_small(0, sums0, head_weight_grad(0, d_own0), gate_sum0, b_out_row0)
     reduce_weights(0)
     forward_weights(1)
     forward_weights(0)
@@ -554,7 +559,7 @@
             vmem((pairs, 4 * hd, two), BF16), vmem(tile, F32), vmem(tile, F32), vmem(tile, F32), vmem((pairs, two, ch), BF16), vmem(tile, BF16),
             vmem((2, rows, n, wide), F32), vmem((n, wide), F32), vmem((n, wide), F32),
             vmem((2, rows, n, n), F32), vmem((group * rows * rows, ch), F32),
-            vmem((5 * hd, ch), F32),
+            vmem((5 * hd, ch), F32), vmem((2, rows, ch, heads * rows), BF16), vmem((pairs, 16, two), BF16),
             vmem((2, heads * rows, n), BF16), vmem((2, group, heads * rows, n), BF16), vmem(piece, BF16), vmem(piece, BF16), vmem(piece, BF16), vmem(piece, BF16),
             vmem((rows, n), BF16), vmem((group, rows, n), BF16), vmem(piece, BF16), vmem(piece, BF16), vmem(piece, BF16),
             vmem((2, group, heads * rows, n), BF16), vmem((2, group, heads * rows, n), BF16),

time: 78.8 us -> 69.4 us (0.88)
  Pallas kernels: 78 us -> 68.7 us
    pallas_call x1, Pallas kernels: 76.9 us -> 67.6 us  [per_device(): pl.pallas_call(functools.partial(kernel, (rows, n, ch, heads, hd, group,...]
where the time goes in v4:
time: 69.4 us; the launch traced here: 69.3 us
  Pallas kernels  68.7 us (99%)
    pallas_call x1, Pallas kernels, per_device(): pl.pallas_call(functools.partial(kernel, (rows, n, ch, heads, hd, group,...  67.6 us

profile of v4, /device:TPU:21, one launch (start us, length us, event | category | flops | bytes accessed | tf_op | source)
XLA Modules:
  0.0 69.3 jit_solution(15431401888121393629)
XLA Ops:
  0.6 67.6 %shard_map.169 = (bf16[16,64,128]{2,1,0:T(8,128)(2,1)S(1)}, bf16[8,128,128]{2,1,0:T(8,128)(2,1)S(1)}, bf16[2,2,8,40,128]{4,3,2,1,0:T(8,128)(2,1)S(1)}, f32[2,16,8,128]{3,2,1,0:T(8,128)S(1)}) custom-call(bf16[8,128,128]{2,1,0:T(8,128)(2,1)} %refs_0_.1, s32[8,128]{1,0:T(8,128)} %refs_1_.1, bf16[8,128,128]{2,1,0:T(8,128)(2,1)} %refs_2_.1, f32[2,128]{1,0:T(2,128)} %refs_3_.1, ...), custom_call_target="tpu_custom_call" | custom-call | tf_op jit(solution)/shard_map/pallas_call | solution.py:573
  68.2 1.1 %shard_map.170 = (bf16[8,128,128]{2,1,0:T(8,128)(2,1)}, bf16[8,128,128]{2,1,0:T(8,128)(2,1)}, f32[2,128]{1,0:T(2,128)}, f32[2,128]{1,0:T(2,128)}, f32[2,128,512]...) custom-call(bf16[16,64,128]{2,1,0:T(8,128)(2,1)S(1)} %get-tuple-element.22, ...), custom_call_target="tpu_custom_call" | custom-call | tf_op jit(solution)/shard_map/pallas_call | solution.py:581

commit v5 on v4

--- a/solution.py
+++ b/solution.py
@@ -119,11 +119,11 @@
     (z_ref, mask_ref, dz_ref, lns_ref, lnb_ref, wp_ref, wb_ref, bg_ref, wo_ref, bo_ref) = local
     load_sems, refs = refs[-1], refs[10:-11]
     (zo_recv, zg_out, w_full, sm_recv,
-     wpt, wot, wbt, wbp, col,
+     wpt, wot, wbt, col,
      xt, xh, inv, a_s, at1, qt, kt, vt, kv, g_s, ot, ut, btmp, qbd, dbd, dot_s, dgt, dpt, dnt, dzt, dmt, dlp, dlt, pf, bias, db, maskb, stage,
      wacc, wsel, dbt,
-     b_send, b_recv, mid_send, mid_recv, dz_send, dz_recv, mk_send, mk_recv, zo_send, dm_send, dm_recv,
-     db_send, db_recv, w_send, w_half, w_mid, w_recv, w_part, sm_send,
+     b_send, b_recv, b1_recv, mid_send, mid_recv, dz_send, dz_recv, mk_send, mk_recv, zo_send, dm_send, dm_recv,
+     db_send, db_recv, d1_send, d1_half, d1_mid, d1_recv, w_send, w_half, w_mid, w_recv, w_part, sm_send, sm_half, sm_mid,
      send_sems, recv_sems) = refs
     me = lax.axis_index(axis)
     core = me % 2
@@ -141,14 +141,19 @@
         return pltpu.make_async_remote_copy(src_ref=send, dst_ref=recv, send_sem=send_sems.at[slot], recv_sem=recv_sems.at[slot],
                                             device_id={axis: me + 1 - 2 * core}, device_id_type=pl.DeviceIdType.MESH)
 
-    ex_b = [exchange(s, b_send.at[s], b_recv.at[s], True) for s in range(2)]
+    ex_b0 = exchange(0, b_send.at[0], b_recv, True)
+    ex_b1 = chip_exchange(1, b_send.at[1], b1_recv.at[core], True)
+    near_b1 = to_sibling(19, b1_recv.at[core], b1_recv.at[core])
     ex_mid = exchange(2, mid_send, mid_recv)
     ex_dz = exchange(3, dz_send, dz_recv)
     ex_mask = exchange(4, mk_send, mk_recv, True)
     ex_zo = exchange(5, zo_send, zo_recv)
     ex_dm = exchange(6, dm_send, dm_recv)
-    ex_db = [exchange(7 + s, db_send.at[s], db_recv.at[s]) for s in range(2)]
-    ex_small = [exchange(9 + s, sm_send.at[s], sm_recv.at[s], True) for s in range(2)]
+    ex_db0 = exchange(7, db_send, db_recv)
+    near_db1 = to_sibling(8, d1_send.at[1 - core], d1_half)
+    ex_db1 = chip_exchange(20, d1_mid, d1_recv)
+    near_small = [to_sibling(9 + s, sm_send.at[s], sm_half.at[s]) for s in range(2)]
+    ex_small = [chip_exchange(21 + s, sm_mid.at[s], sm_recv.at[s], True) for s in range(2)]
     near_w = [to_sibling(11 + s, w_send.at[s, 1 - core], w_half.at[s]) for s in range(2)]
     ex_w = [chip_exchange(13 + s, w_mid.at[s], w_recv.at[s]) for s in range(2)]
     ex_wf = [chip_exchange(15 + s, w_part.at[s], w_full.at[s, core], True) for s in range(2)]
@@ -158,25 +163,33 @@
     for hop in range(1, group):
         pl.semaphore_signal(barrier, inc=1, device_id={axis: lax.rem(me + hop, group)},
                             device_id_type=pl.DeviceIdType.MESH)
-
-    for k in (3, 4, 5, 6, 7, 8, 9):
-        loads[k].wait()
-    head_pick = (lax.broadcasted_iota(jnp.int32, (16, heads), 0) == lax.broadcasted_iota(jnp.int32, (16, heads), 1)).astype(BF16)
-    eye = (lax.broadcasted_iota(jnp.int32, (ch, ch), 0) == lax.broadcasted_iota(jnp.int32, (ch, ch), 1)).astype(BF16)
-    for s in range(2):
-        wpt[s] = wp_ref[s].T
-        wot[s] = wo_ref[s].T
-        w_heads = dot(head_pick, wb_ref[s]).astype(BF16)
-        wbt[s] = w_heads
-        wbp[s] = dot(eye, w_heads, NT).astype(BF16)
-        for place, ref in enumerate((lns_ref, lnb_ref, bg_ref, bo_ref)):
-            col[s, place] = jnp.broadcast_to(ref[s:s + 1, :], (n, ch)).T
 
     def zero_diag(i, carry):
         qbd[i] = jnp.zeros((hd, wide), BF16)
         dbd[i] = jnp.zeros((hd, wide), BF16)
         return carry
     lax.fori_loop(0, rows, zero_diag, 0)
+    for k in (3, 4, 5, 6, 7, 8, 9):
+        loads[k].wait()
+    head_pick = (lax.broadcasted_iota(jnp.int32, (16, heads), 0) == lax.broadcasted_iota(jnp.int32, (16, heads), 1)).astype(BF16)
+    eye = (lax.broadcasted_iota(jnp.int32, (ch, ch), 0) == lax.broadcasted_iota(jnp.int32, (ch, ch), 1)).astype(BF16)
+
+    def prepare(s):
+        wpt[s] = wp_ref[s].T
+        wbt[s] = dot(head_pick, wb_ref[s]).astype(BF16)
+        for place, ref in enumerate((lns_ref, lnb_ref, bg_ref, bo_ref)):
+            col[s, place] = jnp.broadcast_to(ref[s:s + 1, :], (n, ch)).T
+    prepare(0)
+
+    def prepare_late():
+        prepare(1)
+        at16 = lax.broadcasted_iota(jnp.int32, (16, heads * rows), 0)
+        at32 = lax.broadcasted_iota(jnp.int32, (16, heads * rows), 1)
+        for s in range(2):
+            wot[s] = wo_ref[s].T
+            w_heads = dot(eye, wbt[s], NT).astype(BF16)
+            for i in range(rows):
+                wsel[s, i] = dot(w_heads, ((at32 == at16 * rows + i) & (at16 < heads)).astype(BF16)).astype(BF16)
 
     def column(s, place):
         one = col[s, place]
@@ -232,14 +245,22 @@
         for h in range(0, heads, 2):
             some = [btmp[pl.ds(h + r, rows, stride=16), :] for r in range(2)]
             b_send[s, h * rows:(h + 2) * rows, :] = jnp.concatenate(some, axis=0).astype(BF16)
-        ex_b[s].start()
-
-    def take_bias(s):
-        ex_b[s].wait_recv()
-        got = b_recv[s].astype(F32).reshape(group, heads, rows, n)
+        (ex_b0, ex_b1)[s].start()
+
+    def take_bias0():
+        ex_b0.wait_recv()
+        got = b_recv[...].astype(F32).reshape(group, heads, rows, n)
         for h in range(heads):
-            one = got[:, h].reshape(n, n)
-            bias[:, h * n:(h + 1) * n] = (one.T if s == 0 else one) * LOG2E
+            bias[:, h * n:(h + 1) * n] = got[:, h].reshape(n, n).T * LOG2E
+
+    def take_bias1():
+        near_b1.wait_recv()
+        for c in range(2):
+            got = b1_recv[c].astype(F32) * LOG2E
+            for chip in range(chips):
+                for h in range(heads):
+                    at = (2 * chip + c) * rows
+                    bias[at:at + rows, h * n:(h + 1) * n] = got[chip, h * rows:(h + 1) * rows]
 
     def logits(s):
         for i in range(rows):
@@ -322,16 +343,28 @@
         ex_wf[s].wait_recv()
         near_wf[s].start()
 
-    def send_bias_grad(s):
+    def send_bias_grad0():
         for h in range(0, heads, 2):
-            some = [db[:, (h + r) * n:(h + r + 1) * n] for r in range(2)]
-            some = [(one.T if s == 0 else one).reshape(group, rows, n) for one in some]
-            db_send[s, :, h * rows:(h + 2) * rows, :] = jnp.concatenate(some, axis=1).astype(BF16)
-        ex_db[s].start()
+            some = [db[:, (h + r) * n:(h + r + 1) * n].T.reshape(group, rows, n) for r in range(2)]
+            db_send[:, h * rows:(h + 2) * rows, :] = jnp.concatenate(some, axis=1).astype(BF16)
+        ex_db0.start()
+
+    def send_bias_grad1():
+        for h in range(0, heads, 2):
+            some = [db[:, (h + r) * n:(h + r + 1) * n].reshape(chips, 2, rows, n) for r in range(2)]
+            for c in range(2):
+                d1_send[c, :, h * rows:(h + 2) * rows, :] = jnp.concatenate([one[:, c] for one in some], axis=1).astype(BF16)
+        near_db1.start()
+
+    def chip_sum_bias_grad1():
+        near_db1.wait_recv()
+        d1_mid[...] = (d1_send[core].astype(F32) + d1_half[...].astype(F32)).astype(BF16)
+        ex_db1.start()
 
     def take_bias_grad(s):
-        ex_db[s].wait_recv()
-        return jnp.sum(db_recv[s].astype(F32), axis=0).astype(BF16)
+        (ex_db0, ex_db1)[s].wait_recv()
+        got = (db_recv, d1_recv)[s]
+        return jnp.sum(got[...].astype(F32), axis=0).astype(BF16)
 
     def bias_terms(s, d_own):
         return [jnp.concatenate([dot(wsel[s, 2 * t + r], d_own) for r in range(2)], axis=1) for t in range(pairs)]
@@ -365,6 +398,11 @@
         sm_send[s, 2:3, :] = lanes_to_row(gate_sum)
         sm_send[s, 3:4, :] = b_out_row
         sm_send[s, 4:4 + heads, :] = wb_sum[:heads]
+        near_small[s].start()
+
+    def chip_sum_small(s):
+        near_small[s].wait_recv()
+        sm_mid[s] = sm_send[s] + sm_half[s]
         ex_small[s].start()
 
     zero_tile = jnp.zeros((ch, two), F32)
@@ -389,14 +427,10 @@
         dzt[t] = d_y.T
         b_out_row1 = b_out_row1 + jnp.sum(d_y, axis=0, keepdims=True)
     mk_send[...] = mask_ref[...].astype(F32).astype(BF16)
-    ex_dz.start()
+    ex_dz.start(half(0))
     ex_mask.start()
-    at16 = lax.broadcasted_iota(jnp.int32, (16, heads * rows), 0)
-    at32 = lax.broadcasted_iota(jnp.int32, (16, heads * rows), 1)
-    for s in range(2):
-        for i in range(rows):
-            wsel[s, i] = dot(wbp[s], ((at32 == at16 * rows + i) & (at16 < heads)).astype(BF16)).astype(BF16)
-    take_bias(0)
+    prepare_late()
+    take_bias0()
 
     for k, some in enumerate((early, late)):
         attend(0, range(2 * some[0], 2 * some[-1] + 2))
@@ -408,13 +442,8 @@
     for t in range(pairs):
         at1[t] = keep_norm(1, t, xt[1, t])
     send_bias(1)
-
-    ex_dz.wait_recv()
-    unpack(dz_recv)
-    for t in range(pairs):
-        d_low = staged(t).astype(BF16)
-        dlp[t] = d_low
-        dgt[t] = dot(wo_ref[1], d_low, NT)
+    ex_dz.start(half(1))
+
     db[...] = jnp.zeros((n, wide), F32)
     ex_mask.wait_recv()
     whole = mk_recv[...].astype(F32).reshape(n, n).astype(BF16)
@@ -426,24 +455,37 @@
     unpack(mid_recv)
     for t in range(pairs):
         x = staged(t).T
-        g = project(1, t, x, normalize(1, t, x)[0])
-        store_d_o(t, (dgt[t] * g).astype(BF16))
+        project(1, t, x, normalize(1, t, x)[0])
+    ex_b1.wait_recv()
+    near_b1.start()
     logits(1)
-    take_bias(1)
-    attend(1, range(rows))
+    take_bias1()
+    attend(1, range(rows // 2))
+    for t in early:
+        pack(zo_send, t, block_out(1, t).T)
+    ex_zo.start(half(0))
+    attend(1, range(rows // 2, rows))
+    ex_dz.wait_recv()
+    unpack(dz_recv)
+    for t in range(pairs):
+        d_low = staged(t).astype(BF16)
+        dlp[t] = d_low
+        dgt[t] = dot(wo_ref[1], d_low, NT)
+    for t in range(pairs):
+        store_d_o(t, (dgt[t] * g_s[1, t]).astype(BF16))
 
     gate_sum1 = zero_tile
     for k, some in enumerate((early, late)):
         attend_bwd(1, range(2 * some[0], 2 * some[-1] + 2))
+        if k == 1:
+            send_bias_grad1()
         for t in some:
             d_n, gate_sum1 = after_attention(1, t, gate_sum1)
             pack(dm_send, t, d_n.T)
-        if k == 1:
-            send_bias_grad(1)
         ex_dm.start(half(k))
-    for t in range(pairs):
+    for t in late:
         pack(zo_send, t, block_out(1, t).T)
-    ex_zo.start()
+    chip_sum_bias_grad1()
 
     def sum_weights(s):
         top, low = None, None
@@ -456,13 +498,13 @@
     sum_weights(1)
     send_weights(1)
     db[...] = jnp.zeros((n, wide), F32)
-    chip_sum_weights(1)
 
     d_own1 = take_bias_grad(1)
     terms = bias_terms(1, d_own1)
     for t in range(pairs):
         dnt[t] = terms[t]
     ex_dm.wait_recv()
+    chip_sum_weights(1)
     unpack(dm_recv)
     sums1, b_out_sum = (zero_tile, zero_tile), zero_tile
     for t in range(pairs):
@@ -477,16 +519,18 @@
         b_out_sum = b_out_sum + d_y
 
     attend_bwd(0, range(rows))
-    send_bias_grad(0)
+    send_bias_grad0()
     gate_sum0 = zero_tile
     for t in range(pairs):
         dnt[t], gate_sum0 = after_attention(0, t, gate_sum0)
     sum_weights(0)
     send_weights(0)
-    reduce_weights(1)
     send_small(1, sums1, head_weight_grad(1, d_own1), gate_sum1, b_out_row1)
     b_out_row0 = lanes_to_row(b_out_sum)
     chip_sum_weights(0)
+    ex_zo.start(half(1))
+    chip_sum_small(1)
+    reduce_weights(1)
 
     d_own0 = take_bias_grad(0)
     terms = bias_terms(0, d_own0)
@@ -497,13 +541,14 @@
         for r in range(2):
             zg_out[2 * t + r] = d_x[r * n:(r + 1) * n]
     send_small(0, sums0, head_weight_grad(0, d_own0), gate_sum0, b_out_row0)
+    chip_sum_small(0)
     reduce_weights(0)
     forward_weights(1)
     forward_weights(0)
 
     for one in [ex_zo] + ex_small + near_wf:
         one.wait_recv()
-    for one in ex_b + [ex_mid, ex_dz, ex_mask, ex_zo, ex_dm] + ex_db + ex_small + near_w + ex_w + ex_wf + near_wf:
+    for one in [ex_b0, ex_b1, near_b1, ex_mid, ex_dz, ex_mask, ex_zo, ex_dm, ex_db0, near_db1, ex_db1] + near_small + ex_small + near_w + ex_w + ex_wf + near_wf:
         one.wait_send()
 
 
@@ -548,10 +593,10 @@
         out_shape = [jax.ShapeDtypeStruct(a.shape, BF16 if k < 2 else F32) for k, a in enumerate(like)]
         chips = group // 2
         mid_shape = [jax.ShapeDtypeStruct(piece, BF16), jax.ShapeDtypeStruct(z.shape, BF16),
-                     jax.ShapeDtypeStruct((2, 2, chips, w_rows, ch), BF16), jax.ShapeDtypeStruct((2, group, 8, ch), F32)]
+                     jax.ShapeDtypeStruct((2, 2, chips, w_rows, ch), BF16), jax.ShapeDtypeStruct((2, chips, 8, ch), F32)]
         tile = (pairs, ch, two)
         scratch = [
-            vmem((2, 4 * hd, ch), BF16), vmem((2, ch, hd), BF16), vmem((2, 16, ch), BF16), vmem((2, ch, 16), BF16), vmem((2, 4, ch, n), F32),
+            vmem((2, 4 * hd, ch), BF16), vmem((2, ch, hd), BF16), vmem((2, 16, ch), BF16), vmem((2, 4, ch, n), F32),
             vmem((2,) + tile, F32), vmem((2,) + tile, F32), vmem((2, pairs, 8, two), F32), vmem((2, pairs, two, ch), BF16), vmem(tile, BF16),
             vmem((2, pairs, hd, two), BF16), vmem((2, pairs, hd, two), BF16), vmem((2, pairs, hd, two), BF16), vmem((2, pairs, two, 2 * hd), BF16),
             vmem((2, pairs, hd, two), F32), vmem((2, pairs, hd, two), F32), vmem((2, pairs, hd, two), BF16), vmem((rows * 16, n), F32),
@@ -560,12 +605,13 @@
             vmem((2, rows, n, wide), F32), vmem((n, wide), F32), vmem((n, wide), F32),
             vmem((2, rows, n, n), F32), vmem((group * rows * rows, ch), F32),
             vmem((5 * hd, ch), F32), vmem((2, rows, ch, heads * rows), BF16), vmem((pairs, 16, two), BF16),
-            vmem((2, heads * rows, n), BF16), vmem((2, group, heads * rows, n), BF16), vmem(piece, BF16), vmem(piece, BF16), vmem(piece, BF16), vmem(piece, BF16),
+            vmem((2, heads * rows, n), BF16), vmem((group, heads * rows, n), BF16), vmem((2, chips, heads * rows, n), BF16), vmem(piece, BF16), vmem(piece, BF16), vmem(piece, BF16), vmem(piece, BF16),
             vmem((rows, n), BF16), vmem((group, rows, n), BF16), vmem(piece, BF16), vmem(piece, BF16), vmem(piece, BF16),
-            vmem((2, group, heads * rows, n), BF16), vmem((2, group, heads * rows, n), BF16),
+            vmem((group, heads * rows, n), BF16), vmem((group, heads * rows, n), BF16),
+            vmem((2, chips, heads * rows, n), BF16), vmem((chips, heads * rows, n), BF16), vmem((chips, heads * rows, n), BF16), vmem((chips, heads * rows, n), BF16),
             vmem((2, 2, chips, w_rows, ch), BF16), vmem((2, chips, w_rows, ch), BF16), vmem((2, chips, w_rows, ch), BF16), vmem((2, chips, w_rows, ch), BF16),
-            vmem((2, w_rows, ch), BF16), vmem((2, 8, ch), F32),
-            pltpu.SemaphoreType.DMA((19,)), pltpu.SemaphoreType.DMA((19,)),
+            vmem((2, w_rows, ch), BF16), vmem((2, 8, ch), F32), vmem((2, 8, ch), F32), vmem((2, 8, ch), F32),
+            pltpu.SemaphoreType.DMA((23,)), pltpu.SemaphoreType.DMA((23,)),
         ]
         operands = (z, pair_mask, dz_out, ln_scale, ln_shift, w_proj, w_heads, b_gate, w_out, b_out)
         scratch += [vmem(a.shape, a.dtype) for a in operands] + [pltpu.SemaphoreType.DMA((10,))]

time: 69.4 us -> 65.1 us (0.938)
  Pallas kernels: 68.7 us -> 64.4 us
    pallas_call x1, Pallas kernels: 67.6 us -> 63.2 us  [per_device(): pl.pallas_call(functools.partial(kernel, (rows, n, ch, heads, hd, group,...]
where the time goes in v5:
time: 65.1 us; the launch traced here: 65 us
  Pallas kernels  64.4 us (99%)
    pallas_call x1, Pallas kernels, per_device(): pl.pallas_call(functools.partial(kernel, (rows, n, ch, heads, hd, group,...  63.2 us

profile of v5, /device:TPU:21, one launch (start us, length us, event | category | flops | bytes accessed | tf_op | source)
XLA Modules:
  0.0 65.0 jit_solution(673584058844589573)
XLA Ops:
  0.6 63.2 %shard_map.169 = (bf16[16,64,128]{2,1,0:T(8,128)(2,1)S(1)}, bf16[8,128,128]{2,1,0:T(8,128)(2,1)S(1)}, bf16[2,2,8,40,128]{4,3,2,1,0:T(8,128)(2,1)S(1)}, f32[2,8,8,128]{3,2,1,0:T(8,128)S(1)}) custom-call(bf16[8,128,128]{2,1,0:T(8,128)(2,1)} %refs_0_.1, s32[8,128]{1,0:T(8,128)} %refs_1_.1, bf16[8,128,128]{2,1,0:T(8,128)(2,1)} %refs_2_.1, f32[2,128]{1,0:T(2,128)} %refs_3_.1, ...), custom_call_target="tpu_custom_call" | custom-call | tf_op jit(solution)/shard_map/pallas_call | solution.py:619
  63.9 1.1 %shard_map.170 = (bf16[8,128,128]{2,1,0:T(8,128)(2,1)}, bf16[8,128,128]{2,1,0:T(8,128)(2,1)}, f32[2,128]{1,0:T(2,128)}, f32[2,128]{1,0:T(2,128)}, f32[2,128,512]...) custom-call(bf16[16,64,128]{2,1,0:T(8,128)(2,1)S(1)} %get-tuple-element.22, ...), custom_call_target="tpu_custom_call" | custom-call | tf_op jit(solution)/shard_map/pallas_call | solution.py:627

commit v6 on v5

--- a/solution.py
+++ b/solution.py
@@ -317,11 +317,11 @@
         dot_s[t] = d_o
         store_diag(dbd, t, d_o)
 
-    def after_attention(s, t, gate_sum):
+    def gate_grad(s, t, gate_sum):
         g = g_s[s, t]
         d_lin = dgt[t] * ot[s, t] * g * (1.0 - g)
         dpt[t, 3 * hd:, :] = d_lin.astype(BF16)
-        return dot(wp_ref[s], dpt[t]), gate_sum + d_lin
+        return gate_sum + d_lin
 
     def send_weights(s):
         top = wacc[:4 * hd].reshape(2, chips, 4 * hd // group, ch)
@@ -427,9 +427,9 @@
         dzt[t] = d_y.T
         b_out_row1 = b_out_row1 + jnp.sum(d_y, axis=0, keepdims=True)
     mk_send[...] = mask_ref[...].astype(F32).astype(BF16)
+    prepare_late()
     ex_dz.start(half(0))
     ex_mask.start()
-    prepare_late()
     take_bias0()
 
     for k, some in enumerate((early, late)):
@@ -480,8 +480,8 @@
         if k == 1:
             send_bias_grad1()
         for t in some:
-            d_n, gate_sum1 = after_attention(1, t, gate_sum1)
-            pack(dm_send, t, d_n.T)
+            gate_sum1 = gate_grad(1, t, gate_sum1)
+            pack(dm_send, t, dot(wp_ref[1], dpt[t]).T)
         ex_dm.start(half(k))
     for t in late:
         pack(zo_send, t, block_out(1, t).T)
@@ -498,13 +498,14 @@
     sum_weights(1)
     send_weights(1)
     db[...] = jnp.zeros((n, wide), F32)
+    chip_sum_weights(1)
 
     d_own1 = take_bias_grad(1)
     terms = bias_terms(1, d_own1)
     for t in range(pairs):
         dnt[t] = terms[t]
     ex_dm.wait_recv()
-    chip_sum_weights(1)
+    ex_zo.start(half(1))
     unpack(dm_recv)
     sums1, b_out_sum = (zero_tile, zero_tile), zero_tile
     for t in range(pairs):
@@ -517,20 +518,21 @@
         dgt[t] = d_gated
         store_d_o(t, (d_gated * g_s[0, t]).astype(BF16))
         b_out_sum = b_out_sum + d_y
+    gate_sum0 = zero_tile
+    for t in range(pairs):
+        gate_sum0 = gate_grad(0, t, gate_sum0)
 
     attend_bwd(0, range(rows))
     send_bias_grad0()
-    gate_sum0 = zero_tile
-    for t in range(pairs):
-        dnt[t], gate_sum0 = after_attention(0, t, gate_sum0)
     sum_weights(0)
     send_weights(0)
+    for t in range(pairs):
+        dnt[t] = dot(wp_ref[0], dpt[t])
     send_small(1, sums1, head_weight_grad(1, d_own1), gate_sum1, b_out_row1)
     b_out_row0 = lanes_to_row(b_out_sum)
     chip_sum_weights(0)
-    ex_zo.start(half(1))
+    reduce_weights(1)
     chip_sum_small(1)
-    reduce_weights(1)
 
     d_own0 = take_bias_grad(0)
     terms = bias_terms(0, d_own0)

time: 65.1 us -> 63.5 us (0.975)
  Pallas kernels: 64.4 us -> 62.7 us
    pallas_call x1, Pallas kernels: 63.2 us -> 61.6 us  [per_device(): pl.pallas_call(functools.partial(kernel, (rows, n, ch, heads, hd, group,...]
where the time goes in v6:
time: 63.5 us; the launch traced here: 63.4 us
  Pallas kernels  62.7 us (99%)
  between operations  0.65 us (1%)
    pallas_call x1, Pallas kernels, per_device(): pl.pallas_call(functools.partial(kernel, (rows, n, ch, heads, hd, group,...  61.6 us

profile of v6, /device:TPU:21, one launch (start us, length us, event | category | flops | bytes accessed | tf_op | source)
XLA Modules:
  0.0 63.4 jit_solution(9262865999572681229)
XLA Ops:
  0.6 61.6 %shard_map.169 = (bf16[16,64,128]{2,1,0:T(8,128)(2,1)S(1)}, bf16[8,128,128]{2,1,0:T(8,128)(2,1)S(1)}, bf16[2,2,8,40,128]{4,3,2,1,0:T(8,128)(2,1)S(1)}, f32[2,8,8,128]{3,2,1,0:T(8,128)S(1)}) custom-call(bf16[8,128,128]{2,1,0:T(8,128)(2,1)} %refs_0_.1, s32[8,128]{1,0:T(8,128)} %refs_1_.1, bf16[8,128,128]{2,1,0:T(8,128)(2,1)} %refs_2_.1, f32[2,128]{1,0:T(2,128)} %refs_3_.1, ...), custom_call_target="tpu_custom_call" | custom-call | tf_op jit(solution)/shard_map/pallas_call | solution.py:621
  62.3 1.1 %shard_map.170 = (bf16[8,128,128]{2,1,0:T(8,128)(2,1)}, bf16[8,128,128]{2,1,0:T(8,128)(2,1)}, f32[2,128]{1,0:T(2,128)}, f32[2,128]{1,0:T(2,128)}, f32[2,128,512]...) custom-call(bf16[16,64,128]{2,1,0:T(8,128)(2,1)S(1)} %get-tuple-element.22, ...), custom_call_target="tpu_custom_call" | custom-call | tf_op jit(solution)/shard_map/pallas_call | solution.py:629

commit v7 on v6

--- a/solution.py
+++ b/solution.py
@@ -120,7 +120,7 @@
     load_sems, refs = refs[-1], refs[10:-11]
     (zo_recv, zg_out, w_full, sm_recv,
      wpt, wot, wbt, col,
-     xt, xh, inv, a_s, at1, qt, kt, vt, kv, g_s, ot, ut, btmp, qbd, dbd, dot_s, dgt, dpt, dnt, dzt, dmt, dlp, dlt, pf, bias, db, maskb, stage,
+     xt, xh, inv, a_s, at0, at1, qt, kt, vt, kv, g_s, ot, ut, btmp, qbd, dbd, dot_s, dgt, dpt, dnt, dzt, dmt, dlp, dlt, pf, bias, db, maskb, stage,
      wacc, wsel, dbt,
      b_send, b_recv, b1_recv, mid_send, mid_recv, dz_send, dz_recv, mk_send, mk_recv, zo_send, dm_send, dm_recv,
      db_send, db_recv, d1_send, d1_half, d1_mid, d1_recv, w_send, w_half, w_mid, w_recv, w_part, sm_send, sm_half, sm_mid,
@@ -128,8 +128,8 @@
     me = lax.axis_index(axis)
     core = me % 2
     loads = [pltpu.make_async_copy(src, dst, load_sems.at[k]) for k, (src, dst) in enumerate(zip(operands, local))]
-    for one in loads:
-        one.start()
+    for k in (3, 4, 6, 0, 5, 7, 1, 2, 8, 9):
+        loads[k].start()
 
     def exchange(slot, send, recv, same=False):
         return Exchange(group, axis, send, recv, send_sems.at[slot], recv_sems.at[slot], same)
@@ -169,20 +169,30 @@
         dbd[i] = jnp.zeros((hd, wide), BF16)
         return carry
     lax.fori_loop(0, rows, zero_diag, 0)
-    for k in (3, 4, 5, 6, 7, 8, 9):
+    for k in (3, 4, 6):
         loads[k].wait()
     head_pick = (lax.broadcasted_iota(jnp.int32, (16, heads), 0) == lax.broadcasted_iota(jnp.int32, (16, heads), 1)).astype(BF16)
     eye = (lax.broadcasted_iota(jnp.int32, (ch, ch), 0) == lax.broadcasted_iota(jnp.int32, (ch, ch), 1)).astype(BF16)
 
-    def prepare(s):
+    def to_column(s, place):
+        ref = (lns_ref, lnb_ref, bg_ref, bo_ref)[place]
+        col[s, place] = jnp.broadcast_to(ref[s:s + 1, :], (n, ch)).T
+
+    def prepare_norm(s):
+        wbt[s] = dot(head_pick, wb_ref[s]).astype(BF16)
+        to_column(s, 0)
+        to_column(s, 1)
+    prepare_norm(0)
+
+    def prepare_project(s):
         wpt[s] = wp_ref[s].T
-        wbt[s] = dot(head_pick, wb_ref[s]).astype(BF16)
-        for place, ref in enumerate((lns_ref, lnb_ref, bg_ref, bo_ref)):
-            col[s, place] = jnp.broadcast_to(ref[s:s + 1, :], (n, ch)).T
-    prepare(0)
+        to_column(s, 2)
 
     def prepare_late():
-        prepare(1)
+        prepare_norm(1)
+        prepare_project(1)
+        to_column(0, 3)
+        to_column(1, 3)
         at16 = lax.broadcasted_iota(jnp.int32, (16, heads * rows), 0)
         at32 = lax.broadcasted_iota(jnp.int32, (16, heads * rows), 1)
         for s in range(2):
@@ -227,8 +237,7 @@
         btmp[pl.ds(pl.multiple_of(t * 32, 32), 32), :] = jnp.concatenate([b_t[:, :n], b_t[:, n:]], axis=0)
         return a_t
 
-    def project(s, t, x, a_t):
-        xt[s, t] = x
+    def project(s, t, a_t):
         a = a_t.T
         a_s[s, t] = a
         p = dot(wpt[s], a_t).astype(BF16)
@@ -411,15 +420,22 @@
     loads[0].wait()
     for t in range(pairs):
         x = jnp.concatenate([z_ref[2 * t + r].astype(F32).T for r in range(2)], axis=1)
-        project(0, t, x, keep_norm(0, t, x))
+        xt[0, t] = x
+        at0[t] = keep_norm(0, t, x)
     pl.semaphore_wait(barrier, group - 1)
     send_bias(0)
+    loads[5].wait()
+    loads[7].wait()
+    prepare_project(0)
+    for t in range(pairs):
+        project(0, t, at0[t])
     loads[1].wait()
     fill_rows = (mask_ref[...].astype(F32) - 1.0) * (MASK_FILL * LOG2E)
     for i in range(rows):
         maskb[0, i] = jnp.broadcast_to(fill_rows[i:i + 1, :], (n, n)).T
     logits(0)
-    loads[2].wait()
+    for k in (2, 8, 9):
+        loads[k].wait()
     b_out_row1 = jnp.zeros((1, ch), F32)
     for t in range(pairs):
         d_y = jnp.concatenate([dz_ref[2 * t + r].astype(F32) for r in range(2)], axis=0)
@@ -455,7 +471,8 @@
     unpack(mid_recv)
     for t in range(pairs):
         x = staged(t).T
-        project(1, t, x, normalize(1, t, x)[0])
+        xt[1, t] = x
+        project(1, t, normalize(1, t, x)[0])
     ex_b1.wait_recv()
     near_b1.start()
     logits(1)
@@ -599,7 +616,7 @@
         tile = (pairs, ch, two)
         scratch = [
             vmem((2, 4 * hd, ch), BF16), vmem((2, ch, hd), BF16), vmem((2, 16, ch), BF16), vmem((2, 4, ch, n), F32),
-            vmem((2,) + tile, F32), vmem((2,) + tile, F32), vmem((2, pairs, 8, two), F32), vmem((2, pairs, two, ch), BF16), vmem(tile, BF16),
+            vmem((2,) + tile, F32), vmem((2,) + tile, F32), vmem((2, pairs, 8, two), F32), vmem((2, pairs, two, ch), BF16), vmem(tile, BF16), vmem(tile, BF16),
             vmem((2, pairs, hd, two), BF16), vmem((2, pairs, hd, two), BF16), vmem((2, pairs, hd, two), BF16), vmem((2, pairs, two, 2 * hd), BF16),
             vmem((2, pairs, hd, two), F32), vmem((2, pairs, hd, two), F32), vmem((2, pairs, hd, two), BF16), vmem((rows * 16, n), F32),
             vmem((rows, hd, wide), BF16), vmem((rows, hd, wide), BF16), vmem((pairs, hd, two), BF16), vmem((pairs, hd, two), F32),

time: 63.5 us -> 63.4 us (level); the launches traced: 63.4 us -> 62.6 us
  Pallas kernels: 62.7 us -> 61.9 us
    pallas_call x1, Pallas kernels: 61.6 us -> 60.8 us  [per_device(): pl.pallas_call(functools.partial(kernel, (rows, n, ch, heads, hd, group,...]
where the time goes in v7:
time: 63.4 us; the launch traced here: 62.6 us
  Pallas kernels  61.9 us (98%)
  between operations  0.65 us (1%)
    pallas_call x1, Pallas kernels, per_device(): pl.pallas_call(functools.partial(kernel, (rows, n, ch, heads, hd, group,...  60.8 us

profile of v7, /device:TPU:21, one launch (start us, length us, event | category | flops | bytes accessed | tf_op | source)
XLA Modules:
  0.0 62.6 jit_solution(11563430376504025183)
XLA Ops:
  0.6 60.8 %shard_map.169 = (bf16[16,64,128]{2,1,0:T(8,128)(2,1)S(1)}, bf16[8,128,128]{2,1,0:T(8,128)(2,1)S(1)}, bf16[2,2,8,40,128]{4,3,2,1,0:T(8,128)(2,1)S(1)}, f32[2,8,8,128]{3,2,1,0:T(8,128)S(1)}) custom-call(bf16[8,128,128]{2,1,0:T(8,128)(2,1)} %refs_0_.1, s32[8,128]{1,0:T(8,128)} %refs_1_.1, bf16[8,128,128]{2,1,0:T(8,128)(2,1)} %refs_2_.1, f32[2,128]{1,0:T(2,128)} %refs_3_.1, ...), custom_call_target="tpu_custom_call" | custom-call | tf_op jit(solution)/shard_map/pallas_call | solution.py:638
  61.5 1.1 %shard_map.170 = (bf16[8,128,128]{2,1,0:T(8,128)(2,1)}, bf16[8,128,128]{2,1,0:T(8,128)(2,1)}, f32[2,128]{1,0:T(2,128)}, f32[2,128]{1,0:T(2,128)}, f32[2,128,512]...) custom-call(bf16[16,64,128]{2,1,0:T(8,128)(2,1)S(1)} %get-tuple-element.22, ...), custom_call_target="tpu_custom_call" | custom-call | tf_op jit(solution)/shard_map/pallas_call | solution.py:646

commit v8 on v7

--- a/solution.py
+++ b/solution.py
@@ -20,6 +20,13 @@
     return lax.dot_general(a, b, dims, preferred_element_type=F32)
 
 
+def far_first(size):
+    order = [size // 2]
+    for hop in range(size // 2 - 1, 0, -1):
+        order += [hop, size - hop]
+    return order
+
+
 class Exchange:
     def __init__(self, group, axis, send, recv, send_sem, recv_sem, same=False):
         self.group, self.axis, self.send, self.recv = group, axis, send, recv
@@ -27,11 +34,7 @@
 
     def start(self, part=None):
         me = lax.axis_index(self.axis)
-        half = self.group // 2
-        order = [half]
-        for hop in range(half - 1, 0, -1):
-            order += [hop, self.group - hop]
-        for hop in order:
+        for hop in far_first(self.group):
             peer = lax.rem(me + hop, self.group)
             source = self.send if self.same else self.send.at[peer] if part is None else self.send.at[peer, part]
             pltpu.make_async_remote_copy(
@@ -73,10 +76,7 @@
     def start(self):
         me = lax.axis_index(self.axis)
         chip, core = me // 2, me % 2
-        order = [self.chips // 2]
-        for hop in range(self.chips // 2 - 1, 0, -1):
-            order += [hop, self.chips - hop]
-        for hop in order:
+        for hop in far_first(self.chips):
             to = lax.rem(chip + hop, self.chips)
             pltpu.make_async_remote_copy(
                 src_ref=self.send if self.same else self.send.at[to],
@@ -123,10 +123,14 @@
      xt, xh, inv, a_s, at0, at1, qt, kt, vt, kv, g_s, ot, ut, btmp, qbd, dbd, dot_s, dgt, dpt, dnt, dzt, dmt, dlp, dlt, pf, bias, db, maskb, stage,
      wacc, wsel, dbt,
      b_send, b_recv, b1_recv, mid_send, mid_recv, dz_send, dz_recv, mk_send, mk_recv, zo_send, dm_send, dm_recv,
-     db_send, db_recv, d1_send, d1_half, d1_mid, d1_recv, w_send, w_half, w_mid, w_recv, w_part, sm_send, sm_half, sm_mid,
+     db_send, db_half, db_mid, db_recv, w_send, w_half, w_mid, w_recv, w_part, sm_send, sm_half, sm_mid,
      send_sems, recv_sems) = refs
     me = lax.axis_index(axis)
     core = me % 2
+    barrier = pltpu.get_barrier_semaphore()
+    for hop in far_first(group):
+        pl.semaphore_signal(barrier, inc=1, device_id={axis: lax.rem(me + hop, group)},
+                            device_id_type=pl.DeviceIdType.MESH)
     loads = [pltpu.make_async_copy(src, dst, load_sems.at[k]) for k, (src, dst) in enumerate(zip(operands, local))]
     for k in (3, 4, 6, 0, 5, 7, 1, 2, 8, 9):
         loads[k].start()
@@ -149,20 +153,14 @@
     ex_mask = exchange(4, mk_send, mk_recv, True)
     ex_zo = exchange(5, zo_send, zo_recv)
     ex_dm = exchange(6, dm_send, dm_recv)
-    ex_db0 = exchange(7, db_send, db_recv)
-    near_db1 = to_sibling(8, d1_send.at[1 - core], d1_half)
-    ex_db1 = chip_exchange(20, d1_mid, d1_recv)
+    near_db = [to_sibling(7 + s, db_send.at[s, 1 - core], db_half.at[s]) for s in range(2)]
+    ex_db = [chip_exchange((20, 23)[s], db_mid.at[s], db_recv.at[s]) for s in range(2)]
     near_small = [to_sibling(9 + s, sm_send.at[s], sm_half.at[s]) for s in range(2)]
     ex_small = [chip_exchange(21 + s, sm_mid.at[s], sm_recv.at[s], True) for s in range(2)]
     near_w = [to_sibling(11 + s, w_send.at[s, 1 - core], w_half.at[s]) for s in range(2)]
     ex_w = [chip_exchange(13 + s, w_mid.at[s], w_recv.at[s]) for s in range(2)]
     ex_wf = [chip_exchange(15 + s, w_part.at[s], w_full.at[s, core], True) for s in range(2)]
     near_wf = [to_sibling(17 + s, w_full.at[s, core], w_full.at[s, core]) for s in range(2)]
-
-    barrier = pltpu.get_barrier_semaphore()
-    for hop in range(1, group):
-        pl.semaphore_signal(barrier, inc=1, device_id={axis: lax.rem(me + hop, group)},
-                            device_id_type=pl.DeviceIdType.MESH)
 
     def zero_diag(i, carry):
         qbd[i] = jnp.zeros((hd, wide), BF16)
@@ -220,8 +218,8 @@
         parts = [value[r * n:(r + 1) * n].reshape(group, n // group, ch) for r in range(2)]
         send[:, pl.ds(pl.multiple_of(t * 16, 16), 16), :] = jnp.concatenate(parts, axis=1).astype(BF16)
 
-    def half(k):
-        return pl.ds(k * rows * rows // 2, rows * rows // 2)
+    def part_of(some):
+        return pl.ds(2 * some[0] * rows, 2 * len(some) * rows)
 
     def normalize(s, t, x):
         centred = x - jnp.mean(x, axis=0, keepdims=True)
@@ -352,28 +350,22 @@
         ex_wf[s].wait_recv()
         near_wf[s].start()
 
-    def send_bias_grad0():
+    def send_bias_grad(s):
         for h in range(0, heads, 2):
-            some = [db[:, (h + r) * n:(h + r + 1) * n].T.reshape(group, rows, n) for r in range(2)]
-            db_send[:, h * rows:(h + 2) * rows, :] = jnp.concatenate(some, axis=1).astype(BF16)
-        ex_db0.start()
-
-    def send_bias_grad1():
-        for h in range(0, heads, 2):
-            some = [db[:, (h + r) * n:(h + r + 1) * n].reshape(chips, 2, rows, n) for r in range(2)]
+            some = [db[:, (h + r) * n:(h + r + 1) * n] for r in range(2)]
+            some = [(one.T if s == 0 else one).reshape(chips, 2, rows, n) for one in some]
             for c in range(2):
-                d1_send[c, :, h * rows:(h + 2) * rows, :] = jnp.concatenate([one[:, c] for one in some], axis=1).astype(BF16)
-        near_db1.start()
-
-    def chip_sum_bias_grad1():
-        near_db1.wait_recv()
-        d1_mid[...] = (d1_send[core].astype(F32) + d1_half[...].astype(F32)).astype(BF16)
-        ex_db1.start()
+                db_send[s, c, :, h * rows:(h + 2) * rows, :] = jnp.concatenate([one[:, c] for one in some], axis=1).astype(BF16)
+        near_db[s].start()
+
+    def chip_sum_bias_grad(s):
+        near_db[s].wait_recv()
+        db_mid[s] = (db_send[s, core].astype(F32) + db_half[s].astype(F32)).astype(BF16)
+        ex_db[s].start()
 
     def take_bias_grad(s):
-        (ex_db0, ex_db1)[s].wait_recv()
-        got = (db_recv, d1_recv)[s]
-        return jnp.sum(got[...].astype(F32), axis=0).astype(BF16)
+        ex_db[s].wait_recv()
+        return jnp.sum(db_recv[s].astype(F32), axis=0).astype(BF16)
 
     def bias_terms(s, d_own):
         return [jnp.concatenate([dot(wsel[s, 2 * t + r], d_own) for r in range(2)], axis=1) for t in range(pairs)]
@@ -429,12 +421,7 @@
     prepare_project(0)
     for t in range(pairs):
         project(0, t, at0[t])
-    loads[1].wait()
-    fill_rows = (mask_ref[...].astype(F32) - 1.0) * (MASK_FILL * LOG2E)
-    for i in range(rows):
-        maskb[0, i] = jnp.broadcast_to(fill_rows[i:i + 1, :], (n, n)).T
-    logits(0)
-    for k in (2, 8, 9):
+    for k in (1, 2):
         loads[k].wait()
     b_out_row1 = jnp.zeros((1, ch), F32)
     for t in range(pairs):
@@ -443,22 +430,28 @@
         dzt[t] = d_y.T
         b_out_row1 = b_out_row1 + jnp.sum(d_y, axis=0, keepdims=True)
     mk_send[...] = mask_ref[...].astype(F32).astype(BF16)
+    ex_dz.start(part_of(early))
+    ex_mask.start()
+    fill_rows = (mask_ref[...].astype(F32) - 1.0) * (MASK_FILL * LOG2E)
+    for i in range(rows):
+        maskb[0, i] = jnp.broadcast_to(fill_rows[i:i + 1, :], (n, n)).T
+    logits(0)
+    loads[8].wait()
+    loads[9].wait()
     prepare_late()
-    ex_dz.start(half(0))
-    ex_mask.start()
     take_bias0()
 
-    for k, some in enumerate((early, late)):
+    for some in (range(1), range(1, pairs)):
         attend(0, range(2 * some[0], 2 * some[-1] + 2))
         for t in some:
             y = block_out(0, t)
             pack(mid_send, t, y.T)
             xt[1, t] = y.astype(BF16).astype(F32)
-        ex_mid.start(half(k))
+        ex_mid.start(part_of(some))
     for t in range(pairs):
         at1[t] = keep_norm(1, t, xt[1, t])
     send_bias(1)
-    ex_dz.start(half(1))
+    ex_dz.start(part_of(late))
 
     db[...] = jnp.zeros((n, wide), F32)
     ex_mask.wait_recv()
@@ -480,7 +473,7 @@
     attend(1, range(rows // 2))
     for t in early:
         pack(zo_send, t, block_out(1, t).T)
-    ex_zo.start(half(0))
+    ex_zo.start(part_of(early))
     attend(1, range(rows // 2, rows))
     ex_dz.wait_recv()
     unpack(dz_recv)
@@ -495,14 +488,14 @@
     for k, some in enumerate((early, late)):
         attend_bwd(1, range(2 * some[0], 2 * some[-1] + 2))
         if k == 1:
-            send_bias_grad1()
+            send_bias_grad(1)
         for t in some:
             gate_sum1 = gate_grad(1, t, gate_sum1)
             pack(dm_send, t, dot(wp_ref[1], dpt[t]).T)
-        ex_dm.start(half(k))
+        ex_dm.start(part_of(some))
     for t in late:
         pack(zo_send, t, block_out(1, t).T)
-    chip_sum_bias_grad1()
+    chip_sum_bias_grad(1)
 
     def sum_weights(s):
         top, low = None, None
@@ -516,13 +509,13 @@
     send_weights(1)
     db[...] = jnp.zeros((n, wide), F32)
     chip_sum_weights(1)
+    ex_zo.start(part_of(late))
 
     d_own1 = take_bias_grad(1)
     terms = bias_terms(1, d_own1)
     for t in range(pairs):
         dnt[t] = terms[t]
     ex_dm.wait_recv()
-    ex_zo.start(half(1))
     unpack(dm_recv)
     sums1, b_out_sum = (zero_tile, zero_tile), zero_tile
     for t in range(pairs):
@@ -540,9 +533,10 @@
         gate_sum0 = gate_grad(0, t, gate_sum0)
 
     attend_bwd(0, range(rows))
-    send_bias_grad0()
+    send_bias_grad(0)
     sum_weights(0)
     send_weights(0)
+    chip_sum_bias_grad(0)
     for t in range(pairs):
         dnt[t] = dot(wp_ref[0], dpt[t])
     send_small(1, sums1, head_weight_grad(1, d_own1), gate_sum1, b_out_row1)
@@ -567,7 +561,7 @@
 
     for one in [ex_zo] + ex_small + near_wf:
         one.wait_recv()
-    for one in [ex_b0, ex_b1, near_b1, ex_mid, ex_dz, ex_mask, ex_zo, ex_dm, ex_db0, near_db1, ex_db1] + near_small + ex_small + near_w + ex_w + ex_wf + near_wf:
+    for one in [ex_b0, ex_b1, near_b1, ex_mid, ex_dz, ex_mask, ex_zo, ex_dm] + near_db + ex_db + near_small + ex_small + near_w + ex_w + ex_wf + near_wf:
         one.wait_send()
 
 
@@ -626,11 +620,10 @@
             vmem((5 * hd, ch), F32), vmem((2, rows, ch, heads * rows), BF16), vmem((pairs, 16, two), BF16),
             vmem((2, heads * rows, n), BF16), vmem((group, heads * rows, n), BF16), vmem((2, chips, heads * rows, n), BF16), vmem(piece, BF16), vmem(piece, BF16), vmem(piece, BF16), vmem(piece, BF16),
             vmem((rows, n), BF16), vmem((group, rows, n), BF16), vmem(piece, BF16), vmem(piece, BF16), vmem(piece, BF16),
-            vmem((group, heads * rows, n), BF16), vmem((group, heads * rows, n), BF16),
-            vmem((2, chips, heads * rows, n), BF16), vmem((chips, heads * rows, n), BF16), vmem((chips, heads * rows, n), BF16), vmem((chips, heads * rows, n), BF16),
+            vmem((2, 2, chips, heads * rows, n), BF16), vmem((2, chips, heads * rows, n), BF16), vmem((2, chips, heads * rows, n), BF16), vmem((2, chips, heads * rows, n), BF16),
             vmem((2, 2, chips, w_rows, ch), BF16), vmem((2, chips, w_rows, ch), BF16), vmem((2, chips, w_rows, ch), BF16), vmem((2, chips, w_rows, ch), BF16),
             vmem((2, w_rows, ch), BF16), vmem((2, 8, ch), F32), vmem((2, 8, ch), F32), vmem((2, 8, ch), F32),
-            pltpu.SemaphoreType.DMA((23,)), pltpu.SemaphoreType.DMA((23,)),
+            pltpu.SemaphoreType.DMA((24,)), pltpu.SemaphoreType.DMA((24,)),
         ]
         operands = (z, pair_mask, dz_out, ln_scale, ln_shift, w_proj, w_heads, b_gate, w_out, b_out)
         scratch += [vmem(a.shape, a.dtype) for a in operands] + [pltpu.SemaphoreType.DMA((10,))]

time: 63.4 us -> 63.1 us (level); the launches traced: 62.6 us -> 63 us
  no operation moved by 1% of the time
where the time goes in v8:
time: 63.1 us; the launch traced here: 63 us
  Pallas kernels  62.4 us (99%)
  between operations  0.65 us (1%)
    pallas_call x1, Pallas kernels, per_device(): pl.pallas_call(functools.partial(kernel, (rows, n, ch, heads, hd, group,...  61.3 us

profile of v8, /device:TPU:21, one launch (start us, length us, event | category | flops | bytes accessed | tf_op | source)
XLA Modules:
  0.0 63.0 jit_solution(3920209332089102707)
XLA Ops:
  0.6 61.3 %shard_map.169 = (bf16[16,64,128]{2,1,0:T(8,128)(2,1)S(1)}, bf16[8,128,128]{2,1,0:T(8,128)(2,1)S(1)}, bf16[2,2,8,40,128]{4,3,2,1,0:T(8,128)(2,1)S(1)}, f32[2,8,8,128]{3,2,1,0:T(8,128)S(1)}) custom-call(bf16[8,128,128]{2,1,0:T(8,128)(2,1)} %refs_0_.1, s32[8,128]{1,0:T(8,128)} %refs_1_.1, bf16[8,128,128]{2,1,0:T(8,128)(2,1)} %refs_2_.1, f32[2,128]{1,0:T(2,128)} %refs_3_.1, ...), custom_call_target="tpu_custom_call" | custom-call | tf_op jit(solution)/shard_map/pallas_call | solution.py:631
  61.9 1.1 %shard_map.170 = (bf16[8,128,128]{2,1,0:T(8,128)(2,1)}, bf16[8,128,128]{2,1,0:T(8,128)(2,1)}, f32[2,128]{1,0:T(2,128)}, f32[2,128]{1,0:T(2,128)}, f32[2,128,512]...) custom-call(bf16[16,64,128]{2,1,0:T(8,128)(2,1)S(1)} %get-tuple-element.22, ...), custom_call_target="tpu_custom_call" | custom-call | tf_op jit(solution)/shard_map/pallas_call | solution.py:639

commit v9 on v8

--- a/solution.py
+++ b/solution.py
@@ -218,6 +218,9 @@
         parts = [value[r * n:(r + 1) * n].reshape(group, n // group, ch) for r in range(2)]
         send[:, pl.ds(pl.multiple_of(t * 16, 16), 16), :] = jnp.concatenate(parts, axis=1).astype(BF16)
 
+    def pair(t):
+        return slice(t * two, (t + 1) * two)
+
     def part_of(some):
         return pl.ds(2 * some[0] * rows, 2 * len(some) * rows)
 
@@ -237,7 +240,7 @@
 
     def project(s, t, a_t):
         a = a_t.T
-        a_s[s, t] = a
+        a_s[s, pair(t), :] = a
         p = dot(wpt[s], a_t).astype(BF16)
         qt[s, t] = p[:hd]
         kt[s, t] = p[hd:2 * hd]
@@ -291,7 +294,7 @@
 
     def block_out(s, t):
         u = (ot[s, t] * g_s[s, t]).astype(BF16)
-        ut[s, t] = u
+        ut[s, :, pair(t)] = u
         return xt[s, t] + dot(wot[s], u) + column(s, 3)
 
     def attend_bwd(s, some):
@@ -305,6 +308,7 @@
             if k + 1 < len(some):
                 ahead = d_probs(some[k + 1])
             at = slice(r * n, (r + 1) * n)
+            here = slice(i * n, (i + 1) * n)
             for h in range(heads):
                 cols = slice(h * n, (h + 1) * n)
                 p = pf[s, i, :, cols]
@@ -316,9 +320,9 @@
                 d_q = dot(kt[s, t, hs, at], d_s)
                 d_k = dot(qt[s, t, hs, at], d_s, NT)
                 d_v = dot(dot_s[t, hs, at], p.astype(BF16), NT)
-                dpt[t, h * hdim:(h + 1) * hdim, at] = d_q.astype(BF16)
-                dpt[t, hd + h * hdim:hd + (h + 1) * hdim, at] = d_k.astype(BF16)
-                dpt[t, 2 * hd + h * hdim:2 * hd + (h + 1) * hdim, at] = d_v.astype(BF16)
+                dpt[h * hdim:(h + 1) * hdim, here] = d_q.astype(BF16)
+                dpt[hd + h * hdim:hd + (h + 1) * hdim, here] = d_k.astype(BF16)
+                dpt[2 * hd + h * hdim:2 * hd + (h + 1) * hdim, here] = d_v.astype(BF16)
 
     def store_d_o(t, d_o):
         dot_s[t] = d_o
@@ -327,7 +331,7 @@
     def gate_grad(s, t, gate_sum):
         g = g_s[s, t]
         d_lin = dgt[t] * ot[s, t] * g * (1.0 - g)
-        dpt[t, 3 * hd:, :] = d_lin.astype(BF16)
+        dpt[3 * hd:, pair(t)] = d_lin.astype(BF16)
         return gate_sum + d_lin
 
     def send_weights(s):
@@ -375,12 +379,8 @@
         at32 = lax.broadcasted_iota(jnp.int32, (16, heads * rows), 1)
         for t in range(pairs):
             rows_of = [dot((at32 == at16 * rows + (2 * t + r)).astype(BF16), d_own) for r in range(2)]
-            dbt[t] = jnp.concatenate(rows_of, axis=1).astype(BF16)
-        total = None
-        for t in range(pairs):
-            one = dot(dbt[t], a_s[0, t]) if s == 0 else dot(dbt[t], at1[t], NT)
-            total = one if total is None else total + one
-        return total
+            dbt[:, pair(t)] = jnp.concatenate(rows_of, axis=1).astype(BF16)
+        return dot(dbt[...], a_s[0]) if s == 0 else dot(dbt[...], at1[...], NT)
 
     def norm_bwd(s, t, d_n, sums):
         x_hat = xh[s, t]
@@ -449,7 +449,7 @@
             xt[1, t] = y.astype(BF16).astype(F32)
         ex_mid.start(part_of(some))
     for t in range(pairs):
-        at1[t] = keep_norm(1, t, xt[1, t])
+        at1[:, pair(t)] = keep_norm(1, t, xt[1, t])
     send_bias(1)
     ex_dz.start(part_of(late))
 
@@ -479,7 +479,7 @@
     unpack(dz_recv)
     for t in range(pairs):
         d_low = staged(t).astype(BF16)
-        dlp[t] = d_low
+        dlp[pair(t), :] = d_low
         dgt[t] = dot(wo_ref[1], d_low, NT)
     for t in range(pairs):
         store_d_o(t, (dgt[t] * g_s[1, t]).astype(BF16))
@@ -491,39 +491,34 @@
             send_bias_grad(1)
         for t in some:
             gate_sum1 = gate_grad(1, t, gate_sum1)
-            pack(dm_send, t, dot(wp_ref[1], dpt[t]).T)
+            pack(dm_send, t, dot(wp_ref[1], dpt[:, pair(t)]).T)
         ex_dm.start(part_of(some))
     for t in late:
         pack(zo_send, t, block_out(1, t).T)
     chip_sum_bias_grad(1)
 
     def sum_weights(s):
-        top, low = None, None
-        for t in range(pairs):
-            one = dot(dpt[t], a_s[s, t])
-            two_ = dot(ut[1, t], dlp[t]) if s == 1 else dot(ut[0, t], dlt[t], NT)
-            top, low = (one, two_) if top is None else (top + one, low + two_)
-        wacc[:4 * hd] = top
-        wacc[4 * hd:] = low
+        wacc[:4 * hd] = dot(dpt[...], a_s[s])
+        wacc[4 * hd:] = dot(ut[1], dlp[...]) if s == 1 else dot(ut[0], dlt[...], NT)
     sum_weights(1)
     send_weights(1)
     db[...] = jnp.zeros((n, wide), F32)
     chip_sum_weights(1)
     ex_zo.start(part_of(late))
 
+    ex_dm.wait_recv()
+    unpack(dm_recv)
+    for t in range(pairs):
+        dnt[t] = staged(t).T
     d_own1 = take_bias_grad(1)
     terms = bias_terms(1, d_own1)
-    for t in range(pairs):
-        dnt[t] = terms[t]
-    ex_dm.wait_recv()
-    unpack(dm_recv)
     sums1, b_out_sum = (zero_tile, zero_tile), zero_tile
     for t in range(pairs):
-        d_in, sums1 = norm_bwd(1, t, staged(t).T + dnt[t], sums1)
+        d_in, sums1 = norm_bwd(1, t, dnt[t] + terms[t], sums1)
         d_y = d_in + dzt[t]
         dmt[t] = d_y
         d_low = d_y.astype(BF16)
-        dlt[t] = d_low
+        dlt[:, pair(t)] = d_low
         d_gated = dot(wo_ref[0], d_low)
         dgt[t] = d_gated
         store_d_o(t, (d_gated * g_s[0, t]).astype(BF16))
@@ -538,7 +533,7 @@
     send_weights(0)
     chip_sum_bias_grad(0)
     for t in range(pairs):
-        dnt[t] = dot(wp_ref[0], dpt[t])
+        dnt[t] = dot(wp_ref[0], dpt[:, pair(t)])
     send_small(1, sums1, head_weight_grad(1, d_own1), gate_sum1, b_out_row1)
     b_out_row0 = lanes_to_row(b_out_sum)
     chip_sum_weights(0)
@@ -610,14 +605,14 @@
         tile = (pairs, ch, two)
         scratch = [
             vmem((2, 4 * hd, ch), BF16), vmem((2, ch, hd), BF16), vmem((2, 16, ch), BF16), vmem((2, 4, ch, n), F32),
-            vmem((2,) + tile, F32), vmem((2,) + tile, F32), vmem((2, pairs, 8, two), F32), vmem((2, pairs, two, ch), BF16), vmem(tile, BF16), vmem(tile, BF16),
+            vmem((2,) + tile, F32), vmem((2,) + tile, F32), vmem((2, pairs, 8, two), F32), vmem((2, pairs * two, ch), BF16), vmem(tile, BF16), vmem((ch, pairs * two), BF16),
             vmem((2, pairs, hd, two), BF16), vmem((2, pairs, hd, two), BF16), vmem((2, pairs, hd, two), BF16), vmem((2, pairs, two, 2 * hd), BF16),
-            vmem((2, pairs, hd, two), F32), vmem((2, pairs, hd, two), F32), vmem((2, pairs, hd, two), BF16), vmem((rows * 16, n), F32),
+            vmem((2, pairs, hd, two), F32), vmem((2, pairs, hd, two), F32), vmem((2, hd, pairs * two), BF16), vmem((rows * 16, n), F32),
             vmem((rows, hd, wide), BF16), vmem((rows, hd, wide), BF16), vmem((pairs, hd, two), BF16), vmem((pairs, hd, two), F32),
-            vmem((pairs, 4 * hd, two), BF16), vmem(tile, F32), vmem(tile, F32), vmem(tile, F32), vmem((pairs, two, ch), BF16), vmem(tile, BF16),
+            vmem((4 * hd, pairs * two), BF16), vmem(tile, F32), vmem(tile, F32), vmem(tile, F32), vmem((pairs * two, ch), BF16), vmem((ch, pairs * two), BF16),
             vmem((2, rows, n, wide), F32), vmem((n, wide), F32), vmem((n, wide), F32),
             vmem((2, rows, n, n), F32), vmem((group * rows * rows, ch), F32),
-            vmem((5 * hd, ch), F32), vmem((2, rows, ch, heads * rows), BF16), vmem((pairs, 16, two), BF16),
+            vmem((5 * hd, ch), F32), vmem((2, rows, ch, heads * rows), BF16), vmem((16, pairs * two), BF16),
             vmem((2, heads * rows, n), BF16), vmem((group, heads * rows, n), BF16), vmem((2, chips, heads * rows, n), BF16), vmem(piece, BF16), vmem(piece, BF16), vmem(piece, BF16), vmem(piece, BF16),
             vmem((rows, n), BF16), vmem((group, rows, n), BF16), vmem(piece, BF16), vmem(piece, BF16), vmem(piece, BF16),
             vmem((2, 2, chips, heads * rows, n), BF16), vmem((2, chips, heads * rows, n), BF16), vmem((2, chips, heads * rows, n), BF16), vmem((2, chips, heads * rows, n), BF16),

time: 63.1 us -> 63.1 us (level)
  no operation moved by 1% of the time
where the time goes in v9:
time: 63.1 us; the launch traced here: 63 us
  Pallas kernels  62.4 us (99%)
  between operations  0.65 us (1%)
    pallas_call x1, Pallas kernels, per_device(): pl.pallas_call(functools.partial(kernel, (rows, n, ch, heads, hd, group,...  61.3 us

profile of v9, /device:TPU:21, one launch (start us, length us, event | category | flops | bytes accessed | tf_op | source)
XLA Modules:
  0.0 63.0 jit_solution(8998567182722757016)
XLA Ops:
  0.6 61.3 %shard_map.169 = (bf16[16,64,128]{2,1,0:T(8,128)(2,1)S(1)}, bf16[8,128,128]{2,1,0:T(8,128)(2,1)S(1)}, bf16[2,2,8,40,128]{4,3,2,1,0:T(8,128)(2,1)S(1)}, f32[2,8,8,128]{3,2,1,0:T(8,128)S(1)}) custom-call(bf16[8,128,128]{2,1,0:T(8,128)(2,1)} %refs_0_.1, s32[8,128]{1,0:T(8,128)} %refs_1_.1, bf16[8,128,128]{2,1,0:T(8,128)(2,1)} %refs_2_.1, f32[2,128]{1,0:T(2,128)} %refs_3_.1, ...), custom_call_target="tpu_custom_call" | custom-call | tf_op jit(solution)/shard_map/pallas_call | solution.py:626
  61.9 1.1 %shard_map.170 = (bf16[8,128,128]{2,1,0:T(8,128)(2,1)}, bf16[8,128,128]{2,1,0:T(8,128)(2,1)}, f32[2,128]{1,0:T(2,128)}, f32[2,128]{1,0:T(2,128)}, f32[2,128,512]...) custom-call(bf16[16,64,128]{2,1,0:T(8,128)(2,1)S(1)} %get-tuple-element.22, ...), custom_call_target="tpu_custom_call" | custom-call | tf_op jit(solution)/shard_map/pallas_call | solution.py:634

commit v10 on v9

--- a/solution.py
+++ b/solution.py
@@ -157,10 +157,12 @@
     ex_db = [chip_exchange((20, 23)[s], db_mid.at[s], db_recv.at[s]) for s in range(2)]
     near_small = [to_sibling(9 + s, sm_send.at[s], sm_half.at[s]) for s in range(2)]
     ex_small = [chip_exchange(21 + s, sm_mid.at[s], sm_recv.at[s], True) for s in range(2)]
-    near_w = [to_sibling(11 + s, w_send.at[s, 1 - core], w_half.at[s]) for s in range(2)]
-    ex_w = [chip_exchange(13 + s, w_mid.at[s], w_recv.at[s]) for s in range(2)]
-    ex_wf = [chip_exchange(15 + s, w_part.at[s], w_full.at[s, core], True) for s in range(2)]
-    near_wf = [to_sibling(17 + s, w_full.at[s, core], w_full.at[s, core]) for s in range(2)]
+    per = hd // group
+    sets = [(1, pl.ds(0, 5 * per)), (0, pl.ds(0, 3 * per)), (0, pl.ds(3 * per, 2 * per))]
+    near_w = [to_sibling(11 + k, w_send.at[s, 1 - core, :, at], w_half.at[s, :, at]) for k, (s, at) in enumerate(sets)]
+    ex_w = [chip_exchange(14 + k, w_mid.at[s, :, at], w_recv.at[s, :, at]) for k, (s, at) in enumerate(sets)]
+    ex_wf = [chip_exchange(24 + k, w_part.at[s, at], w_full.at[s, core, :, at], True) for k, (s, at) in enumerate(sets)]
+    near_wf = [to_sibling((17, 18, 27)[k], w_full.at[s, core, :, at], w_full.at[s, core, :, at]) for k, (s, at) in enumerate(sets)]
 
     def zero_diag(i, carry):
         qbd[i] = jnp.zeros((hd, wide), BF16)
@@ -334,25 +336,28 @@
         dpt[3 * hd:, pair(t)] = d_lin.astype(BF16)
         return gate_sum + d_lin
 
-    def send_weights(s):
-        top = wacc[:4 * hd].reshape(2, chips, 4 * hd // group, ch)
-        low = wacc[4 * hd:].reshape(2, chips, hd // group, ch)
-        w_send[s] = jnp.concatenate([top, low], axis=2).astype(BF16)
-        near_w[s].start()
-
-    def chip_sum_weights(s):
-        near_w[s].wait_recv()
-        w_mid[s] = (w_send[s, core].astype(F32) + w_half[s].astype(F32)).astype(BF16)
-        ex_w[s].start()
-
-    def reduce_weights(s):
-        ex_w[s].wait_recv()
-        w_part[s] = jnp.sum(w_recv[s].astype(F32), axis=0).astype(BF16)
-        ex_wf[s].start()
-
-    def forward_weights(s):
-        ex_wf[s].wait_recv()
-        near_wf[s].start()
+    def send_weights(k):
+        s, at = sets[k]
+        parts = [(0, 3 * hd), (3 * hd, hd), (4 * hd, hd)]
+        for low, size in (parts, parts[:1], parts[1:])[k]:
+            w_send[s, :, :, pl.ds(low // group, size // group), :] = wacc[low:low + size].reshape(2, chips, size // group, ch).astype(BF16)
+        near_w[k].start()
+
+    def chip_sum_weights(k):
+        s, at = sets[k]
+        near_w[k].wait_recv()
+        w_mid[s, :, at, :] = (w_send[s, core, :, at, :].astype(F32) + w_half[s, :, at, :].astype(F32)).astype(BF16)
+        ex_w[k].start()
+
+    def reduce_weights(k):
+        s, at = sets[k]
+        ex_w[k].wait_recv()
+        w_part[s, at, :] = jnp.sum(w_recv[s, :, at, :].astype(F32), axis=0).astype(BF16)
+        ex_wf[k].start()
+
+    def forward_weights(k):
+        ex_wf[k].wait_recv()
+        near_wf[k].start()
 
     def send_bias_grad(s):
         for h in range(0, heads, 2):
@@ -497,13 +502,11 @@
         pack(zo_send, t, block_out(1, t).T)
     chip_sum_bias_grad(1)
 
-    def sum_weights(s):
-        wacc[:4 * hd] = dot(dpt[...], a_s[s])
-        wacc[4 * hd:] = dot(ut[1], dlp[...]) if s == 1 else dot(ut[0], dlt[...], NT)
-    sum_weights(1)
-    send_weights(1)
+    wacc[:4 * hd] = dot(dpt[...], a_s[1])
+    wacc[4 * hd:] = dot(ut[1], dlp[...])
+    send_weights(0)
     db[...] = jnp.zeros((n, wide), F32)
-    chip_sum_weights(1)
+    chip_sum_weights(0)
     ex_zo.start(part_of(late))
 
     ex_dm.wait_recv()
@@ -526,18 +529,22 @@
     gate_sum0 = zero_tile
     for t in range(pairs):
         gate_sum0 = gate_grad(0, t, gate_sum0)
+    wacc[3 * hd:4 * hd] = dot(dpt[3 * hd:], a_s[0])
+    wacc[4 * hd:] = dot(ut[0], dlt[...], NT)
+    send_weights(2)
 
     attend_bwd(0, range(rows))
     send_bias_grad(0)
-    sum_weights(0)
-    send_weights(0)
+    wacc[:3 * hd] = dot(dpt[:3 * hd], a_s[0])
+    send_weights(1)
     chip_sum_bias_grad(0)
+    chip_sum_weights(2)
     for t in range(pairs):
         dnt[t] = dot(wp_ref[0], dpt[:, pair(t)])
     send_small(1, sums1, head_weight_grad(1, d_own1), gate_sum1, b_out_row1)
     b_out_row0 = lanes_to_row(b_out_sum)
-    chip_sum_weights(0)
-    reduce_weights(1)
+    chip_sum_weights(1)
+    reduce_weights(0)
     chip_sum_small(1)
 
     d_own0 = take_bias_grad(0)
@@ -549,10 +556,12 @@
         for r in range(2):
             zg_out[2 * t + r] = d_x[r * n:(r + 1) * n]
     send_small(0, sums0, head_weight_grad(0, d_own0), gate_sum0, b_out_row0)
+    reduce_weights(2)
     chip_sum_small(0)
-    reduce_weights(0)
+    reduce_weights(1)
+    forward_weights(0)
+    forward_weights(2)
     forward_weights(1)
-    forward_weights(0)
 
     for one in [ex_zo] + ex_small + near_wf:
         one.wait_recv()
@@ -567,11 +576,12 @@
     stage[...] = zo_ref[...].astype(F32).reshape(group * rows * rows, ch)
     for i in range(rows):
         zo_out[i] = stage[pl.ds(i, n, stride=rows), :].astype(BF16)
-    cut = 4 * hd // group
+    per = hd // group
     for s in range(2):
         full = w_ref[s].astype(F32).reshape(group, 5 * hd // group, ch)
-        wp_out[s] = full[:, :cut].reshape(4 * hd, ch).T
-        wo_out[s] = full[:, cut:].reshape(hd, ch)
+        wp_out[s, :, :3 * hd] = full[:, :3 * per].reshape(3 * hd, ch).T
+        wp_out[s, :, 3 * hd:] = full[:, 3 * per:4 * per].reshape(hd, ch).T
+        wo_out[s] = full[:, 4 * per:].reshape(hd, ch)
         total = jnp.sum(sm_ref[s], axis=0)
         for place, ref in enumerate((lns_out, lnb_out, bg_out, bo_out)):
             ref[s:s + 1, :] = total[place:place + 1, :]
@@ -618,7 +628,7 @@
             vmem((2, 2, chips, heads * rows, n), BF16), vmem((2, chips, heads * rows, n), BF16), vmem((2, chips, heads * rows, n), BF16), vmem((2, chips, heads * rows, n), BF16),
             vmem((2, 2, chips, w_rows, ch), BF16), vmem((2, chips, w_rows, ch), BF16), vmem((2, chips, w_rows, ch), BF16), vmem((2, chips, w_rows, ch), BF16),
             vmem((2, w_rows, ch), BF16), vmem((2, 8, ch), F32), vmem((2, 8, ch), F32), vmem((2, 8, ch), F32),
-            pltpu.SemaphoreType.DMA((24,)), pltpu.SemaphoreType.DMA((24,)),
+            pltpu.SemaphoreType.DMA((28,)), pltpu.SemaphoreType.DMA((28,)),
         ]
         operands = (z, pair_mask, dz_out, ln_scale, ln_shift, w_proj, w_heads, b_gate, w_out, b_out)
         scratch += [vmem(a.shape, a.dtype) for a in operands] + [pltpu.SemaphoreType.DMA((10,))]

time: 63.1 us -> 64 us (1.014)
  Pallas kernels: 62.4 us -> 63.2 us
    pallas_call x1, Pallas kernels: 61.3 us -> 62.1 us  [per_device(): pl.pallas_call(functools.partial(kernel, (rows, n, ch, heads, hd, group,...]
where the time goes in v10:
time: 64 us; the launch traced here: 63.9 us
  Pallas kernels  63.2 us (99%)
  between operations  0.65 us (1%)
    pallas_call x1, Pallas kernels, per_device(): pl.pallas_call(functools.partial(kernel, (rows, n, ch, heads, hd, group,...  62.1 us

profile of v10, /device:TPU:21, one launch (start us, length us, event | category | flops | bytes accessed | tf_op | source)
XLA Modules:
  0.0 63.9 jit_solution(3615686739974089429)
XLA Ops:
  0.6 62.1 %shard_map.169 = (bf16[16,64,128]{2,1,0:T(8,128)(2,1)S(1)}, bf16[8,128,128]{2,1,0:T(8,128)(2,1)S(1)}, bf16[2,2,8,40,128]{4,3,2,1,0:T(8,128)(2,1)S(1)}, f32[2,8,8,128]{3,2,1,0:T(8,128)S(1)}) custom-call(bf16[8,128,128]{2,1,0:T(8,128)(2,1)} %refs_0_.1, s32[8,128]{1,0:T(8,128)} %refs_1_.1, bf16[8,128,128]{2,1,0:T(8,128)(2,1)} %refs_2_.1, f32[2,128]{1,0:T(2,128)} %refs_3_.1, ...), custom_call_target="tpu_custom_call" | custom-call | tf_op jit(solution)/shard_map/pallas_call | solution.py:636
  62.8 1.1 %shard_map.170 = (bf16[8,128,128]{2,1,0:T(8,128)(2,1)}, bf16[8,128,128]{2,1,0:T(8,128)(2,1)}, f32[2,128]{1,0:T(2,128)}, f32[2,128]{1,0:T(2,128)}, f32[2,128,512]...) custom-call(bf16[16,64,128]{2,1,0:T(8,128)(2,1)S(1)} %get-tuple-element.22, ...), custom_call_target="tpu_custom_call" | custom-call | tf_op jit(solution)/shard_map/pallas_call | solution.py:644

commit v11 on v9

--- a/solution.py
+++ b/solution.py
@@ -430,8 +430,6 @@
         dzt[t] = d_y.T
         b_out_row1 = b_out_row1 + jnp.sum(d_y, axis=0, keepdims=True)
     mk_send[...] = mask_ref[...].astype(F32).astype(BF16)
-    ex_dz.start(part_of(early))
-    ex_mask.start()
     fill_rows = (mask_ref[...].astype(F32) - 1.0) * (MASK_FILL * LOG2E)
     for i in range(rows):
         maskb[0, i] = jnp.broadcast_to(fill_rows[i:i + 1, :], (n, n)).T
@@ -439,6 +437,8 @@
     loads[8].wait()
     loads[9].wait()
     prepare_late()
+    ex_dz.start(part_of(early))
+    ex_mask.start()
     take_bias0()
 
     for some in (range(1), range(1, pairs)):

time: 63.1 us -> 63.2 us (level)
  no operation moved by 1% of the time
where the time goes in v11:
time: 63.2 us; the launch traced here: 63.1 us
  Pallas kernels  62.4 us (99%)
  between operations  0.65 us (1%)
    pallas_call x1, Pallas kernels, per_device(): pl.pallas_call(functools.partial(kernel, (rows, n, ch, heads, hd, group,...  61.3 us

profile of v11, /device:TPU:21, one launch (start us, length us, event | category | flops | bytes accessed | tf_op | source)
XLA Modules:
  0.0 63.1 jit_solution(2491656256604851671)
XLA Ops:
  0.6 61.3 %shard_map.169 = (bf16[16,64,128]{2,1,0:T(8,128)(2,1)S(1)}, bf16[8,128,128]{2,1,0:T(8,128)(2,1)S(1)}, bf16[2,2,8,40,128]{4,3,2,1,0:T(8,128)(2,1)S(1)}, f32[2,8,8,128]{3,2,1,0:T(8,128)S(1)}) custom-call(bf16[8,128,128]{2,1,0:T(8,128)(2,1)} %refs_0_.1, s32[8,128]{1,0:T(8,128)} %refs_1_.1, bf16[8,128,128]{2,1,0:T(8,128)(2,1)} %refs_2_.1, f32[2,128]{1,0:T(2,128)} %refs_3_.1, ...), custom_call_target="tpu_custom_call" | custom-call | tf_op jit(solution)/shard_map/pallas_call | solution.py:626
  62.0 1.1 %shard_map.170 = (bf16[8,128,128]{2,1,0:T(8,128)(2,1)}, bf16[8,128,128]{2,1,0:T(8,128)(2,1)}, f32[2,128]{1,0:T(2,128)}, f32[2,128]{1,0:T(2,128)}, f32[2,128,512]...) custom-call(bf16[16,64,128]{2,1,0:T(8,128)(2,1)S(1)} %get-tuple-element.22, ...), custom_call_target="tpu_custom_call" | custom-call | tf_op jit(solution)/shard_map/pallas_call | solution.py:634
